TPU v7x, 32 devices: a whole 2x2x4 slice. The times are simulated.
32 devices in a mesh: group: 2 (over y), tm: 4 (over z), bl: 2 (over x), pol: 2 (over core).
Axes of the slice: x: 2, y: 2, z: 4, core: 2. Of those that a mesh axis runs over, the one named last changes fastest.
Arguments:
- visibilities: bfloat16 [1600, 256, 2, 384], P(('group', 'tm'), ('bl', 'pol')), parts along dimension 0, may hold values from -6 to 6
- flag_mask: int32 [1600], P(('group', 'tm')), parts along dimension 0, may hold values 0 or 1
- kernel_index: int32 [256], P(('bl', 'pol')), may hold values from 0 to 15
- filter_bank: float32 [2, 16, 257], replicated, may hold values from -0.875 to 0.875
Outputs:
- fringe_filtered: bfloat16 [160, 256, 2, 384], P('group', ('bl', 'pol', 'tm')), parts along dimension 0
There are 2 independent parts, one for each index of `group`. A program takes and returns all parts, laid end to end along the dimension named above; an argument that names none is the same for every part. Nothing has to cross between parts.
All inputs are finite; a program needn't handle non-finite values. No bound on the sum of `flag_mask` on one device may be relied on, other than what follows from the above.
Results may differ from a plain program's by a relative error of at most 0.001.
Values may be sent and summed in bfloat16 or wider, within the bound.
A program may use at most 192 MiB of HBM per device.

v0:
```python
import functools

import jax
import jax.numpy as jnp
from jax import lax
from jax.experimental import pallas as pl
from jax.experimental.pallas import tpu as pltpu
from jax.sharding import PartitionSpec as P

TAPS = 257
AVG = 10
HALF = TAPS // 2
SIDE = -(-HALF // AVG)
GROUP = 8


def round_up(value, step):
    return -(-value // step) * step


def row_plan(block_rows):
    out_count = block_rows // AVG
    side_rows = round_up(2 * SIDE, 8)
    local_rows = round_up(2 * out_count, 8)
    highest = 2 * (block_rows + HALF + AVG * SIDE)
    lowest = 2 * HALF - AVG * (2 * out_count + side_rows)
    period = round_up(max(highest, 2 * (TAPS + AVG) - lowest), 128)
    return out_count, side_rows, local_rows, period


def averaged_taps(filter_bank, period):
    width = TAPS + AVG - 1
    padded = jnp.pad(filter_bank, ((0, 0), (0, 0), (AVG - 1, AVG - 1)))
    total = padded[:, :, 0:width]
    for shift in range(1, AVG):
        total = total + padded[:, :, shift : shift + width]
    real, imag = total[0] * (1.0 / AVG), total[1] * (1.0 / AVG)
    to_real = jnp.stack([real, -imag], axis=-1).reshape(-1, 2 * width)
    to_imag = jnp.stack([imag, real], axis=-1).reshape(-1, 2 * width)
    to_real = jnp.pad(to_real, ((0, 0), (0, period - 2 * width)))
    to_imag = jnp.pad(to_imag, ((0, 0), (0, period - 2 * width)))
    return jnp.stack([to_real, jnp.roll(to_imag, -AVG, axis=1)], axis=1)


def build_bands(taps_ref, flag_ref, band_ref, block_rows):
    out_count, side_rows, local_rows, period = row_plan(block_rows)
    total_rows = 2 * side_rows + local_rows
    flags = flag_ref[...].astype(jnp.float32)

    def one_filter(f, carry):
        base = jnp.concatenate([taps_ref[f]] * 4, axis=0)
        tile = pltpu.roll(base, 0, 1, stride=AVG, stride_axis=0)
        start = 0
        for first, rows in (
            (-2 * SIDE, side_rows),
            (0, local_rows),
            (2 * out_count, side_rows),
        ):
            shifts = [(AVG * (first + row) - 2 * HALF) % period for row in range(0, rows, 8)]
            tiles = [pltpu.roll(tile, shift, 1)[:, : 2 * block_rows] for shift in shifts]
            band = jnp.concatenate(tiles, axis=0) * flags
            high = band.astype(jnp.bfloat16)
            low = (band - high.astype(jnp.float32)).astype(jnp.bfloat16)
            band_ref[f, start : start + rows, :] = high
            band_ref[f, total_rows + start : total_rows + start + rows, :] = low
            start += rows
        return carry

    lax.fori_loop(0, taps_ref.shape[0], one_filter, 0, unroll=4)


def band_kernel(taps_ref, flag_ref, band_ref, *, block_rows):
    build_bands(taps_ref, flag_ref, band_ref, block_rows)


def band_call(taps, flags):
    block_rows = flags.shape[1] // 2
    _, side_rows, local_rows, _ = row_plan(block_rows)
    return pl.pallas_call(
        functools.partial(band_kernel, block_rows=block_rows),
        in_specs=[pl.BlockSpec(memory_space=pltpu.VMEM)] * 2,
        out_specs=pl.BlockSpec(memory_space=pltpu.VMEM),
        out_shape=jax.ShapeDtypeStruct(
            (taps.shape[0], 2 * (2 * side_rows + local_rows), 2 * block_rows), jnp.bfloat16
        ),
    )(taps, flags)


def stream_kernel(
    index_ref,
    band_ref,
    vis_ref,
    out_ref,
    slab_ref,
    to_left,
    to_right,
    from_left,
    from_right,
    local_ref,
    sum_ref,
    done_ref,
    load_sem,
    left_send,
    right_send,
    left_recv,
    right_recv,
    done_send,
    done_recv,
    *,
    count,
):
    me = lax.axis_index("tm")
    _, block_rows, group, _, channels = slab_ref.shape
    chunks = done_ref.shape[0]
    per_owner = chunks // count
    out_count, side_rows, local_rows, _ = row_plan(block_rows)
    total_rows = 2 * side_rows + local_rows
    side = 2 * SIDE
    has_left, has_right = me > 0, me < count - 1

    def chunk_at(step):
        turn = step % count
        owner = (turn % 2) * (count - 1 - turn // 2) + (1 - turn % 2) * (turn // 2)
        return owner, step // count

    def load(step):
        owner, part = chunk_at(step)
        first = (owner * per_owner + part) * group
        slot = step % 2
        return pltpu.make_async_copy(
            vis_ref.at[:, pl.ds(first, group)], slab_ref.at[slot], load_sem.at[slot]
        )

    def remote(source, target, send_sem, recv_sem, device):
        return pltpu.make_async_remote_copy(
            src_ref=source,
            dst_ref=target,
            send_sem=send_sem,
            recv_sem=recv_sem,
            device_id={"tm": device},
            device_id_type=pl.DeviceIdType.MESH,
        )

    def leftward(step):
        return remote(
            to_left.at[step],
            from_right.at[step],
            left_send.at[step],
            right_recv.at[step],
            jnp.maximum(me - 1, 0),
        )

    def rightward(step):
        return remote(
            to_right.at[step],
            from_left.at[step],
            right_send.at[step],
            left_recv.at[step],
            jnp.minimum(me + 1, count - 1),
        )

    def placed(source, part):
        return out_ref.at[pl.ds(source * out_count, out_count), pl.ds(part * group, group)]

    def deliver(step):
        owner, part = chunk_at(step)
        return remote(
            done_ref.at[step], placed(me, part), done_send.at[step], done_recv.at[me, part], owner
        )

    def keep(step):
        _, part = chunk_at(step)
        return pltpu.make_async_copy(done_ref.at[step], placed(me, part), done_send.at[step])

    load(0).start()
    barrier = pltpu.get_barrier_semaphore()
    for offset in range(1, count):
        pl.semaphore_signal(
            barrier,
            inc=1,
            device_id={"tm": lax.rem(me + offset, count)},
            device_id_type=pl.DeviceIdType.MESH,
        )
    pl.semaphore_wait(barrier, count - 1)

    def compute(step, carry):
        @pl.when(step + 1 < chunks)
        def _():
            load(step + 1).start()

        load(step).wait()
        owner, part = chunk_at(step)
        first = (owner * per_owner + part) * group
        slot = step % 2
        for i in range(group):
            which = index_ref[first + i]
            slab = slab_ref[slot, :, i].reshape(2 * block_rows, channels)
            both = jnp.dot(band_ref[which], slab, preferred_element_type=jnp.float32)
            rows = both[:total_rows] + both[total_rows:]
            to_left[step, side * i : side * (i + 1), :] = rows[:side]
            local_ref[step, i] = rows[side_rows : side_rows + 2 * out_count]
            start = side_rows + local_rows
            to_right[step, side * i : side * (i + 1), :] = rows[start : start + side]

        @pl.when(has_left)
        def _():
            leftward(step).start()

        @pl.when(has_right)
        def _():
            rightward(step).start()

        return carry

    lax.fori_loop(0, chunks, compute, 0)

    def finish(step, carry):
        @pl.when(has_left)
        def _():
            rightward(step).wait_recv()

        @pl.when(has_right)
        def _():
            leftward(step).wait_recv()

        for i in range(group):
            sum_ref[...] = local_ref[step, i]

            @pl.when(has_left)
            def _():
                sum_ref[:side] += from_left[step, side * i : side * (i + 1), :]

            @pl.when(has_right)
            def _():
                sum_ref[2 * out_count - side :] += from_right[step, side * i : side * (i + 1), :]

            done_ref[step, :, i] = (
                sum_ref[...].astype(jnp.bfloat16).reshape(out_count, 2, channels)
            )
        owner, _ = chunk_at(step)

        @pl.when(owner == me)
        def _():
            keep(step).start()

        @pl.when(owner != me)
        def _():
            deliver(step).start()

        return carry

    lax.fori_loop(0, chunks, finish, 0)

    def drain(step, carry):
        @pl.when(has_left)
        def _():
            leftward(step).wait_send()

        @pl.when(has_right)
        def _():
            rightward(step).wait_send()

        owner, _ = chunk_at(step)

        @pl.when(owner == me)
        def _():
            keep(step).wait()

        @pl.when(owner != me)
        def _():
            deliver(step).wait_send()

        return carry

    lax.fori_loop(0, chunks, drain, 0)

    def collect(turn, carry):
        source = lax.rem(me + 1 + turn, count)
        for part in range(per_owner):
            remote(
                done_ref.at[0],
                placed(source, part),
                done_send.at[0],
                done_recv.at[source, part],
                source,
            ).wait_recv()
        return carry

    lax.fori_loop(0, count - 1, collect, 0)


def stream_call(kernel_index, bands, visibilities):
    block_rows, bases, _, channels = visibilities.shape
    count = lax.axis_size("tm")
    out_count = block_rows // AVG
    owned = bases // count
    group = GROUP
    while owned % group:
        group //= 2
    chunks = bases // group
    edge = pltpu.VMEM((chunks, 2 * SIDE * group, channels), jnp.float32)
    chunk_sems = pltpu.SemaphoreType.DMA((chunks,))
    return pl.pallas_call(
        functools.partial(stream_kernel, count=count),
        in_specs=[
            pl.BlockSpec(memory_space=pltpu.SMEM),
            pl.BlockSpec(memory_space=pltpu.VMEM),
            pl.BlockSpec(memory_space=pl.ANY),
        ],
        out_specs=pl.BlockSpec(memory_space=pl.ANY),
        out_shape=jax.ShapeDtypeStruct((count * out_count, owned, 2, channels), jnp.bfloat16),
        scratch_shapes=[
            pltpu.VMEM((2, block_rows, group, 2, channels), jnp.bfloat16),
            edge,
            edge,
            edge,
            edge,
            pltpu.VMEM((chunks, group, 2 * out_count, channels), jnp.float32),
            pltpu.VMEM((2 * out_count, channels), jnp.float32),
            pltpu.VMEM((chunks, out_count, group, 2, channels), jnp.bfloat16),
            pltpu.SemaphoreType.DMA((2,)),
            chunk_sems,
            chunk_sems,
            chunk_sems,
            chunk_sems,
            chunk_sems,
            pltpu.SemaphoreType.DMA((count, owned // group)),
        ],
        compiler_params=pltpu.CompilerParams(
            collective_id=0, has_side_effects=True, vmem_limit_bytes=50 * 1024 * 1024
        ),
    )(kernel_index, bands, visibilities)


def per_device(visibilities, flag_mask, kernel_index, filter_bank):
    period = row_plan(visibilities.shape[0])[3]
    taps = averaged_taps(filter_bank, period)
    flags = jnp.repeat(flag_mask, 2)[None, :]
    bands = band_call(taps, flags)
    return stream_call(kernel_index, bands, visibilities)


def solution(mesh):
    placed = (
        P(("group", "tm"), ("bl", "pol"), None, None),
        P(("group", "tm")),
        P(("bl", "pol")),
        P(),
    )
    return jax.shard_map(
        per_device,
        mesh=mesh,
        in_specs=placed,
        out_specs=P("group", ("bl", "pol", "tm"), None, None),
        check_vma=False,
    )
```

profile of v0, /device:TPU:8, one launch (start us, length us, event | category | flops | bytes accessed | tf_op | source)
XLA Modules:
  0.0 115.6 jit_solution(3004132474889912696)
XLA Ops:
  0.0 1.6 %slice_add_fusion = f32[2,16,266]{2,1,0:T(8,128)S(1)} fusion(f32[2,16,257]{2,1,0:T(8,128)} %param.7), kind=kLoop, calls=%fused_computation.5 | loop fusion | flops 76608 | bytes 66944 | tf_op jit(solution)/shard_map/add | solution.py:36
  1.6 0.8 broadcast_in_dim.3
  2.4 0.7 broadcast_in_dim_reshape.3.flag_ref
  3.1 0.0 copy-start
  3.1 0.2 copy.7
  3.3 0.2 reshape.37
  3.5 0.1 copy.8
  3.6 0.1 stack.20
  3.7 0.2 copy.9
  3.9 0.2 reshape.38
  4.1 0.1 copy.10
  4.2 0.1 pad_slice_fusion
  4.3 0.1 pad_maximum_fusion.1
  4.5 0.8 pad_maximum_fusion.taps_ref
  5.2 4.7 %shard_map.46.band_ref = bf16[16,208,400]{2,1,0:T(8,128)(2,1)} custom-call(f32[16,2,1024]{2,1,0:T(2,128)} %pad_maximum_fusion.taps_ref, s32[1,400]{1,0:T(1,128)} %broadcast_in_dim_reshape.3.flag_ref), custom_call_target="tpu_custom_call" | custom-call | tf_op jit(solution)/shard_map/pallas_call | solution.py:79
  10.0 0.0 copy-done
  10.0 104.4 %shard_map.47 = bf16[80,16,2,384]{3,2,1,0:T(2,128)(2,1)S(1)} custom-call(s32[64]{0:T(128)S(1)} %copy-done, bf16[16,208,400]{2,1,0:T(8,128)(2,1)} %shard_map.46.band_ref, bf16[200,64,2,384]{3,2,1,0:T(2,128)(2,1)} %vis_ref.1), custom_call_target="tpu_custom_call" | custom-call | tf_op jit(solution)/shard_map/pallas_call | solution.py:303
  114.4 1.3 %copy.13 = bf16[80,16,2,384]{3,2,1,0:T(2,128)(2,1)} copy(bf16[80,16,2,384]{3,2,1,0:T(2,128)(2,1)S(1)} %shard_map.47) | data formatting | bytes 3932160
  (6 shorter events, 0.1 us)
Async XLA Ops:
  3.1 6.8 %copy-start = (s32[64]{0:T(128)S(1)}, s32[64]{0:T(128)}, u32[]{:S(2)}) copy-start(s32[64]{0:T(128)} %index_ref.1) | copy-start | bytes 772
where the time goes:
time: 116 us
  Pallas kernels  109 us (94%)
  local copies, waits for them, and re-layouts  3.99 us (3%)
  other arithmetic  2.43 us (2%)
    pallas_call x1, Pallas kernels, stream_call(): pl.pallas_call(functools.partial(stream_kernel, count=count), in_specs=[p...  104 us
    pallas_call x1, Pallas kernels, band_call(): pl.pallas_call(functools.partial(band_kernel, block_rows=block_rows), in_...  4.72 us

commit v1 on v0

v1 whole, which is shorter than its diff:
```python
import functools

import jax
import jax.numpy as jnp
from jax import lax
from jax.experimental import pallas as pl
from jax.experimental.pallas import tpu as pltpu
from jax.sharding import PartitionSpec as P

TAPS = 257
AVG = 10
HALF = TAPS // 2
SIDE = -(-HALF // AVG)
GROUP = 8
LOADS = 3
LEVELS = 32767.0
TINY = 1e-33


def round_up(value, step):
    return -(-value // step) * step


def row_plan(block_rows):
    out_count = block_rows // AVG
    edge, mid = out_count, 2 * SIDE - out_count
    assert 0 < mid < SIDE <= out_count
    edge_rows, mid_rows = round_up(2 * edge, 8), round_up(2 * mid, 8)
    total_rows = 2 * edge_rows + mid_rows
    highest = 2 * (block_rows + HALF + AVG * SIDE)
    lowest = 2 * HALF - 2 * AVG * (SIDE + edge)
    period = round_up(max(highest, 2 * (TAPS + AVG) - lowest), 128)
    return out_count, edge, mid, edge_rows, mid_rows, total_rows, period


def averaged_taps(filter_bank, period):
    width = TAPS + AVG - 1
    padded = jnp.pad(filter_bank, ((0, 0), (0, 0), (AVG - 1, AVG - 1)))
    total = padded[:, :, 0:width]
    for shift in range(1, AVG):
        total = total + padded[:, :, shift : shift + width]
    real, imag = total[0] * (1.0 / AVG), total[1] * (1.0 / AVG)
    to_real = jnp.stack([real, -imag], axis=-1).reshape(-1, 2 * width)
    to_imag = jnp.stack([imag, real], axis=-1).reshape(-1, 2 * width)
    to_real = jnp.pad(to_real, ((0, 0), (0, period - 2 * width)))
    to_imag = jnp.pad(to_imag, ((0, 0), (0, period - 2 * width)))
    return jnp.stack([to_real, jnp.roll(to_imag, -AVG, axis=1)], axis=1)


def build_bands(taps_ref, flag_ref, band_ref, block_rows):
    out_count, edge, mid, edge_rows, mid_rows, total_rows, period = row_plan(block_rows)
    flags = flag_ref[...].astype(jnp.float32)
    runs = ((-SIDE, edge, edge_rows), (out_count - SIDE, mid, mid_rows), (SIDE, edge, edge_rows))

    def one_filter(f, carry):
        base = jnp.concatenate([taps_ref[f]] * 4, axis=0)
        tile = pltpu.roll(base, 0, 1, stride=AVG, stride_axis=0)
        tiles = []
        for first, count, rows in runs:
            for row in range(0, rows, 8):
                shift = (2 * AVG * first + AVG * row - 2 * HALF) % period
                piece = pltpu.roll(tile, shift, 1)[:, : 2 * block_rows] * flags
                if row + 8 > 2 * count:
                    at = lax.broadcasted_iota(jnp.int32, piece.shape, 0)
                    piece = jnp.where(at < 2 * count - row, piece, 0.0)
                tiles.append(piece)
        band = jnp.concatenate(tiles, axis=0)
        high = band.astype(jnp.bfloat16)
        band_ref[f, :total_rows, :] = high
        band_ref[f, total_rows:, :] = (band - high.astype(jnp.float32)).astype(jnp.bfloat16)
        return carry

    lax.fori_loop(0, taps_ref.shape[0], one_filter, 0, unroll=4)


def band_kernel(taps_ref, flag_ref, band_ref, *, block_rows):
    build_bands(taps_ref, flag_ref, band_ref, block_rows)


def band_call(taps, flags):
    block_rows = flags.shape[1] // 2
    total_rows = row_plan(block_rows)[5]
    return pl.pallas_call(
        functools.partial(band_kernel, block_rows=block_rows),
        in_specs=[pl.BlockSpec(memory_space=pltpu.VMEM)] * 2,
        out_specs=pl.BlockSpec(memory_space=pltpu.VMEM),
        out_shape=jax.ShapeDtypeStruct(
            (taps.shape[0], 2 * total_rows, 2 * block_rows), jnp.bfloat16
        ),
    )(taps, flags)


def encode(value, code_ref, step_ref, i):
    peak = jnp.max(jnp.max(jnp.abs(value), axis=0, keepdims=True), axis=1, keepdims=True)
    peak = jnp.maximum(peak, TINY)
    step_ref[i : i + 1, :] = jnp.broadcast_to(peak * (1.0 / LEVELS), (1, step_ref.shape[1]))
    code = jnp.round(value * (LEVELS / peak)).astype(jnp.int32).astype(jnp.int16)
    code_ref[:, i] = code.reshape(-1, 2, value.shape[1])


def decode(code):
    rows = code.astype(jnp.int32).astype(jnp.float32)
    return rows.reshape(2 * code.shape[0], code.shape[2])


def stream_kernel(
    index_ref,
    band_ref,
    vis_ref,
    out_ref,
    slab_ref,
    sum_ref,
    edge_ref,
    edge_step_ref,
    mid_ref,
    mid_step_ref,
    in_ref,
    in_edge_step_ref,
    in_mid_step_ref,
    done_ref,
    own_ref,
    load_sem,
    edge_send,
    edge_step_send,
    mid_send,
    mid_step_send,
    edge_recv,
    edge_step_recv,
    mid_recv,
    mid_step_recv,
    done_send,
    done_recv,
    own_sem,
    *,
    count,
):
    me = lax.axis_index("tm")
    _, block_rows, group, _, channels = slab_ref.shape
    chunks = done_ref.shape[0]
    per_owner = chunks // count
    out_count, edge, mid, edge_rows, mid_rows, total_rows, _ = row_plan(block_rows)
    alone = out_count - SIDE
    mid_at, far_at = edge_rows, edge_rows + mid_rows
    has_left, has_right = me > 0, me < count - 1
    nearer, farther = jnp.minimum(me, count - 1 - me), jnp.maximum(me, count - 1 - me)
    sign = jnp.where(2 * me <= count - 1, 1, -1)

    def chunk_at(step):
        turn, part = step // per_owner, step % per_owner
        late = turn - (farther - nearer)
        flip = jnp.where(late % 2 == 0, sign, -sign)
        owner = jnp.where(
            late < 0, me + sign * (farther - turn), me + flip * (nearer - late // 2)
        )
        return owner, part, owner * per_owner + part

    def load(step):
        _, _, chunk = chunk_at(step)
        slot = step % LOADS
        return pltpu.make_async_copy(
            vis_ref.at[:, pl.ds(chunk * group, group)], slab_ref.at[slot], load_sem.at[slot]
        )

    def remote(source, target, send_sem, recv_sem, device):
        return pltpu.make_async_remote_copy(
            src_ref=source,
            dst_ref=target,
            send_sem=send_sem,
            recv_sem=recv_sem,
            device_id={"tm": device},
            device_id_type=pl.DeviceIdType.MESH,
        )

    def slot_of(owner, part, chunk, receiver, rightward):
        second = jnp.logical_and(owner == receiver, jnp.logical_not(rightward))
        return jnp.where(second, chunks + part, chunk)

    def edge_copies(chunk, slot, rightward, device):
        start = jnp.where(rightward, mid, 0)
        return (
            remote(
                edge_ref.at[chunk],
                in_ref.at[slot, pl.ds(start, edge)],
                edge_send.at[chunk],
                edge_recv.at[slot],
                device,
            ),
            remote(
                edge_step_ref.at[chunk],
                in_edge_step_ref.at[slot],
                edge_step_send.at[chunk],
                edge_step_recv.at[slot],
                device,
            ),
        )

    def mid_copies(chunk, slot, rightward, device):
        start = jnp.where(rightward, 0, edge)
        return (
            remote(
                mid_ref.at[chunk],
                in_ref.at[slot, pl.ds(start, mid)],
                mid_send.at[chunk],
                mid_recv.at[slot],
                device,
            ),
            remote(
                mid_step_ref.at[chunk],
                in_mid_step_ref.at[slot],
                mid_step_send.at[chunk],
                mid_step_recv.at[slot],
                device,
            ),
        )

    def placed(row, rows, part):
        return out_ref.at[pl.ds(row, rows), pl.ds(part * group, group)]

    def full_done(source, chunk, part, rightward, device):
        row = jnp.where(rightward, out_count * (source - 1) + alone, out_count * source + SIDE)
        return remote(
            done_ref.at[chunk],
            placed(row, edge, part),
            done_send.at[chunk],
            done_recv.at[source, part],
            device,
        )

    def short_done(source, chunk, part, rightward, device):
        row = jnp.where(rightward, 0, out_count * source + SIDE)
        start = jnp.where(rightward, SIDE, 0)
        return remote(
            done_ref.at[chunk, pl.ds(start, alone)],
            placed(row, alone, part),
            done_send.at[chunk],
            done_recv.at[source, part],
            device,
        )

    def keep(part, low, rows):
        return pltpu.make_async_copy(
            own_ref.at[part, pl.ds(low, rows)],
            placed(jnp.maximum(out_count * me - SIDE, 0), rows, part),
            own_sem.at[part],
        )

    for step in range(LOADS - 1):
        load(step).start()
    barrier = pltpu.get_barrier_semaphore()
    for offset in range(1, count):
        pl.semaphore_signal(
            barrier,
            inc=1,
            device_id={"tm": lax.rem(me + offset, count)},
            device_id_type=pl.DeviceIdType.MESH,
        )
    pl.semaphore_wait(barrier, count - 1)

    def flow(owner):
        rightward = owner > me
        upstream = jnp.where(rightward, has_left, has_right)
        return rightward, upstream, jnp.where(rightward, me + 1, me - 1)

    def compute(step, carry):
        @pl.when(step + LOADS - 1 < chunks)
        def _():
            load(step + LOADS - 1).start()

        load(step).wait()
        owner, part, chunk = chunk_at(step)
        slot = step % LOADS
        rightward, upstream, target = flow(owner)
        landing = slot_of(owner, part, chunk, target, rightward)
        for i in range(group):
            which = index_ref[chunk * group + i]
            slab = slab_ref[slot, :, i].reshape(2 * block_rows, channels)
            both = jnp.dot(band_ref[which], slab, preferred_element_type=jnp.float32)
            sum_ref[chunk, i] = both[:total_rows] + both[total_rows:]

        @pl.when(owner != me)
        def _():
            start = pl.multiple_of(jnp.where(rightward, far_at, 0), 8)
            for i in range(group):
                encode(
                    sum_ref[chunk, i, pl.ds(start, 2 * edge), :],
                    edge_ref.at[chunk],
                    edge_step_ref.at[chunk],
                    i,
                )
            for copy in edge_copies(chunk, landing, rightward, target):
                copy.start()

        @pl.when(jnp.logical_and(owner != me, jnp.logical_not(upstream)))
        def _():
            for i in range(group):
                encode(
                    sum_ref[chunk, i, mid_at : mid_at + 2 * mid, :],
                    mid_ref.at[chunk],
                    mid_step_ref.at[chunk],
                    i,
                )
            for copy in mid_copies(chunk, landing, rightward, target):
                copy.start()

        return carry

    lax.fori_loop(0, chunks, compute, 0)

    def step_of(step_ref, slot, i):
        return jnp.concatenate([step_ref[slot, i : i + 1, :]] * (channels // 128), axis=1)

    def finish(step, carry):
        owner, part, chunk = chunk_at(step)
        rightward, upstream, target = flow(owner)
        landing = slot_of(owner, part, chunk, target, rightward)
        forward = owner != me

        @pl.when(jnp.logical_and(forward, upstream))
        def _():
            for copy in edge_copies(chunk, chunk, rightward, target):
                copy.wait_recv()
            start = jnp.where(rightward, edge, 0)
            for i in range(group):
                came = decode(in_ref[chunk, pl.ds(start, mid), i])
                value = sum_ref[chunk, i, mid_at : mid_at + 2 * mid, :]
                value = value + came * step_of(in_edge_step_ref, chunk, i)
                encode(value, mid_ref.at[chunk], mid_step_ref.at[chunk], i)
            for copy in mid_copies(chunk, landing, rightward, target):
                copy.start()
            for copy in mid_copies(chunk, chunk, rightward, target):
                copy.wait_recv()
            start = jnp.where(rightward, 0, mid)
            near = pl.multiple_of(jnp.where(rightward, 0, far_at), 8)
            at = lax.broadcasted_iota(jnp.int32, (2 * edge, channels), 0)
            first = jnp.where(rightward, 0, 2 * (edge - mid))
            of_mid = jnp.logical_and(at >= first, at < first + 2 * mid)
            for i in range(group):
                came = decode(in_ref[chunk, pl.ds(start, edge), i])
                unit = jnp.where(
                    of_mid,
                    step_of(in_mid_step_ref, chunk, i),
                    step_of(in_edge_step_ref, chunk, i),
                )
                value = sum_ref[chunk, i, pl.ds(near, 2 * edge), :] + came * unit
                done_ref[chunk, :, i] = value.astype(jnp.bfloat16).reshape(edge, 2, channels)
            full_done(me, chunk, part, rightward, owner).start()

        @pl.when(jnp.logical_and(forward, jnp.logical_not(upstream)))
        def _():
            near = pl.multiple_of(jnp.where(rightward, 0, far_at), 8)
            for i in range(group):
                value = sum_ref[chunk, i, pl.ds(near, 2 * edge), :]
                done_ref[chunk, :, i] = value.astype(jnp.bfloat16).reshape(edge, 2, channels)
            short_done(me, chunk, part, rightward, owner).start()

        def from_side(slot, rightward, near, edge_start, first):
            for copy in edge_copies(chunk, slot, rightward, me):
                copy.wait_recv()
            for copy in mid_copies(chunk, slot, rightward, me):
                copy.wait_recv()
            at = lax.broadcasted_iota(jnp.int32, (2 * edge, channels), 0)
            of_mid = jnp.logical_and(at >= first, at < first + 2 * mid)
            for i in range(group):
                edge_unit = step_of(in_edge_step_ref, slot, i)
                unit = jnp.where(of_mid, step_of(in_mid_step_ref, slot, i), edge_unit)
                came = decode(in_ref[slot, edge_start : edge_start + edge, i])
                sum_ref[chunk, i, near : near + 2 * edge, :] += came * unit
                start = edge if rightward else 0
                came = decode(in_ref[slot, start : start + mid, i])
                sum_ref[chunk, i, mid_at : mid_at + 2 * mid, :] += came * edge_unit

        @pl.when(jnp.logical_and(owner == me, has_left))
        def _():
            from_side(chunk, True, 0, 0, 0)

        @pl.when(jnp.logical_and(owner == me, has_right))
        def _():
            from_side(chunks + part, False, far_at, mid, 2 * (edge - mid))

        @pl.when(owner == me)
        def _():
            for i in range(group):
                for row, rows, start in (
                    (0, edge, 0),
                    (edge, mid, mid_at),
                    (edge + mid, edge, far_at),
                ):
                    value = sum_ref[chunk, i, start : start + 2 * rows, :].astype(jnp.bfloat16)
                    own_ref[part, row : row + rows, i] = value.reshape(rows, 2, channels)

            @pl.when(jnp.logical_and(has_left, has_right))
            def _():
                keep(part, 0, 2 * edge + mid).start()

            @pl.when(jnp.logical_not(has_left))
            def _():
                keep(part, SIDE, out_count + SIDE).start()

            @pl.when(jnp.logical_not(has_right))
            def _():
                keep(part, 0, out_count + SIDE).start()

        return carry

    lax.fori_loop(0, chunks, finish, 0)

    def drain(step, carry):
        owner, part, chunk = chunk_at(step)
        rightward, upstream, target = flow(owner)

        @pl.when(owner != me)
        def _():
            for copy in edge_copies(chunk, chunk, rightward, target):
                copy.wait_send()
            for copy in mid_copies(chunk, chunk, rightward, target):
                copy.wait_send()

            @pl.when(upstream)
            def _():
                full_done(me, chunk, part, rightward, owner).wait_send()

            @pl.when(jnp.logical_not(upstream))
            def _():
                short_done(me, chunk, part, rightward, owner).wait_send()

        @pl.when(owner == me)
        def _():
            @pl.when(jnp.logical_and(has_left, has_right))
            def _():
                keep(part, 0, 2 * edge + mid).wait()

            @pl.when(jnp.logical_not(jnp.logical_and(has_left, has_right)))
            def _():
                keep(part, 0, out_count + SIDE).wait()

        return carry

    lax.fori_loop(0, chunks, drain, 0)

    def collect(turn, carry):
        source = lax.rem(me + 1 + turn, count)
        end = jnp.logical_or(source == 0, source == count - 1)
        for part in range(per_owner):

            @pl.when(end)
            def _():
                short_done(source, 0, part, source < me, source).wait_recv()

            @pl.when(jnp.logical_not(end))
            def _():
                full_done(source, 0, part, source < me, source).wait_recv()

        return carry

    lax.fori_loop(0, count - 1, collect, 0)


def stream_call(kernel_index, bands, visibilities):
    block_rows, bases, _, channels = visibilities.shape
    count = lax.axis_size("tm")
    out_count, edge, mid, _, _, total_rows, _ = row_plan(block_rows)
    owned = bases // count
    group = GROUP
    while owned % group:
        group //= 2
    chunks, parts = bases // group, owned // group
    slots = chunks + parts
    sent, landed = pltpu.SemaphoreType.DMA((chunks,)), pltpu.SemaphoreType.DMA((slots,))
    return pl.pallas_call(
        functools.partial(stream_kernel, count=count),
        in_specs=[
            pl.BlockSpec(memory_space=pltpu.SMEM),
            pl.BlockSpec(memory_space=pltpu.VMEM),
            pl.BlockSpec(memory_space=pl.ANY),
        ],
        out_specs=pl.BlockSpec(memory_space=pl.ANY),
        out_shape=jax.ShapeDtypeStruct((count * out_count, owned, 2, channels), jnp.bfloat16),
        scratch_shapes=[
            pltpu.VMEM((LOADS, block_rows, group, 2, channels), jnp.bfloat16),
            pltpu.VMEM((chunks, group, total_rows, channels), jnp.float32),
            pltpu.VMEM((chunks, edge, group, 2, channels), jnp.int16),
            pltpu.VMEM((chunks, group, 128), jnp.float32),
            pltpu.VMEM((chunks, mid, group, 2, channels), jnp.int16),
            pltpu.VMEM((chunks, group, 128), jnp.float32),
            pltpu.VMEM((slots, edge + mid, group, 2, channels), jnp.int16),
            pltpu.VMEM((slots, group, 128), jnp.float32),
            pltpu.VMEM((slots, group, 128), jnp.float32),
            pltpu.VMEM((chunks, edge, group, 2, channels), jnp.bfloat16),
            pltpu.VMEM((parts, 2 * edge + mid, group, 2, channels), jnp.bfloat16),
            pltpu.SemaphoreType.DMA((LOADS,)),
            sent,
            sent,
            sent,
            sent,
            landed,
            landed,
            landed,
            landed,
            sent,
            pltpu.SemaphoreType.DMA((count, parts)),
            pltpu.SemaphoreType.DMA((parts,)),
        ],
        compiler_params=pltpu.CompilerParams(
            collective_id=0, has_side_effects=True, vmem_limit_bytes=56 * 1024 * 1024
        ),
    )(kernel_index, bands, visibilities)


def per_device(visibilities, flag_mask, kernel_index, filter_bank):
    period = row_plan(visibilities.shape[0])[6]
    taps = averaged_taps(filter_bank, period)
    flags = jnp.repeat(flag_mask, 2)[None, :]
    bands = band_call(taps, flags)
    return stream_call(kernel_index, bands, visibilities)


def solution(mesh):
    placed = (
        P(("group", "tm"), ("bl", "pol"), None, None),
        P(("group", "tm")),
        P(("bl", "pol")),
        P(),
    )
    return jax.shard_map(
        per_device,
        mesh=mesh,
        in_specs=placed,
        out_specs=P("group", ("bl", "pol", "tm"), None, None),
        check_vma=False,
    )
```

time: 116 us -> 79.3 us (0.68)
  Pallas kernels: 109 us -> 69.6 us
  local copies, waits for them, and re-layouts: 3.99 us -> 6.88 us
    pallas_call x1, Pallas kernels: 104 us -> 64.6 us  [stream_call(): pl.pallas_call(functools.partial(stream_kernel, count=count), in_specs=[p...]
    unnamed x3 -> x1, local copies, waits for them, and re-layouts: 1.28 us -> 4.17 us
where the time goes in v1:
time: 79.3 us; the launch traced here: 79 us
  Pallas kernels  69.6 us (88%)
  local copies, waits for them, and re-layouts  6.88 us (9%)
  other arithmetic  2.43 us (3%)
    pallas_call x1, Pallas kernels, stream_call(): pl.pallas_call(functools.partial(stream_kernel, count=count), in_specs=[p...  64.6 us
    pallas_call x1, Pallas kernels, band_call(): pl.pallas_call(functools.partial(band_kernel, block_rows=block_rows), in_...  5.04 us
    unnamed x1, local copies, waits for them, and re-layouts  4.17 us

profile of v1, /device:TPU:8, one launch (start us, length us, event | category | flops | bytes accessed | tf_op | source)
XLA Modules:
  0.0 79.0 jit_solution(6288424087827544977)
XLA Ops:
  0.0 1.6 %slice_add_fusion = f32[2,16,266]{2,1,0:T(8,128)S(1)} fusion(f32[2,16,257]{2,1,0:T(8,128)} %param.7), kind=kLoop, calls=%fused_computation.5 | loop fusion | flops 76608 | bytes 66944 | tf_op jit(solution)/shard_map/add | solution.py:41
  1.6 0.8 broadcast_in_dim.3
  2.4 0.7 broadcast_in_dim_reshape.3.flag_ref
  3.1 0.2 copy.7
  3.3 0.2 reshape.37
  3.5 0.1 copy.8
  3.6 0.1 stack.20
  3.7 0.2 copy.9
  3.9 0.2 reshape.38
  4.1 0.1 copy.10
  4.2 0.1 pad_slice_fusion
  4.3 0.1 pad_maximum_fusion.1
  4.5 0.8 pad_maximum_fusion.taps_ref
  5.2 5.0 %shard_map.46.band_ref = bf16[16,192,400]{2,1,0:T(8,128)(2,1)} custom-call(f32[16,2,1024]{2,1,0:T(2,128)} %pad_maximum_fusion.taps_ref, s32[1,400]{1,0:T(1,128)} %broadcast_in_dim_reshape.3.flag_ref), custom_call_target="tpu_custom_call" | custom-call | tf_op jit(solution)/shard_map/pallas_call | solution.py:83
  10.3 64.6 %shard_map.47 = bf16[80,16,2,384]{3,2,1,0:T(2,128)(2,1)} custom-call(s32[64]{0:T(128)} %index_ref.1, bf16[16,192,400]{2,1,0:T(8,128)(2,1)} %shard_map.46.band_ref, bf16[200,64,2,384]{3,2,1,0:T(2,128)(2,1)} %vis_ref.1), custom_call_target="tpu_custom_call" | custom-call | tf_op jit(solution)/shard_map/pallas_call | solution.py:469
  74.9 4.2 %copy.13 = bf16[80,16,2,384]{3,2,1,0:T(2,128)(2,1)} copy(bf16[80,16,2,384]{3,2,1,0:T(2,128)(2,1)} %shard_map.47) | data formatting | bytes 3932160
  (6 shorter events, 0.1 us)

commit v2 on v1

--- a/solution.py
+++ b/solution.py
@@ -33,33 +33,69 @@
     return out_count, edge, mid, edge_rows, mid_rows, total_rows, period
 
 
-def averaged_taps(filter_bank, period):
-    width = TAPS + AVG - 1
-    padded = jnp.pad(filter_bank, ((0, 0), (0, 0), (AVG - 1, AVG - 1)))
-    total = padded[:, :, 0:width]
-    for shift in range(1, AVG):
-        total = total + padded[:, :, shift : shift + width]
-    real, imag = total[0] * (1.0 / AVG), total[1] * (1.0 / AVG)
-    to_real = jnp.stack([real, -imag], axis=-1).reshape(-1, 2 * width)
-    to_imag = jnp.stack([imag, real], axis=-1).reshape(-1, 2 * width)
-    to_real = jnp.pad(to_real, ((0, 0), (0, period - 2 * width)))
-    to_imag = jnp.pad(to_imag, ((0, 0), (0, period - 2 * width)))
-    return jnp.stack([to_real, jnp.roll(to_imag, -AVG, axis=1)], axis=1)
-
-
-def build_bands(taps_ref, flag_ref, band_ref, block_rows):
+def spread_taps(bank_ref):
+    filters, taps = bank_ref.shape[1:]
+    width = round_up(2 * (taps + AVG), 128)
+    parts = []
+    for part in (bank_ref[0], bank_ref[1]):
+        for _ in range(3):
+            parts.append(part.astype(jnp.bfloat16))
+            part = part - parts[-1].astype(jnp.float32)
+    ahead = lax.broadcasted_iota(jnp.int32, (taps, width), 1)
+    ahead = ahead - 2 * lax.broadcasted_iota(jnp.int32, (taps, width), 0)
+    hit = jnp.logical_and(jnp.logical_and(ahead >= 0, ahead < 2 * AVG), ahead % 2 == 0)
+    spread = jnp.where(hit, 1.0, 0.0).astype(jnp.bfloat16)
+    total = jnp.dot(jnp.concatenate(parts, axis=0), spread, preferred_element_type=jnp.float32)
+    total = [total[filters * k : filters * (k + 1)] for k in range(6)]
+    real = (total[0] + total[1] + total[2]) * (1.0 / AVG)
+    imag = (total[3] + total[4] + total[5]) * (1.0 / AVG)
+    return real - pltpu.roll(imag, 1, 1), imag + pltpu.roll(real, 1, 1)
+
+
+def spread_flags(flag_ref, block_rows):
+    flags = jnp.broadcast_to(flag_ref[...], (8, block_rows)).astype(jnp.float32)
+    ahead = lax.broadcasted_iota(jnp.int32, (block_rows, 2 * block_rows), 1)
+    ahead = ahead - 2 * lax.broadcasted_iota(jnp.int32, (block_rows, 2 * block_rows), 0)
+    hit = jnp.logical_and(ahead >= 0, ahead < 2)
+    spread = jnp.where(hit, 1.0, 0.0).astype(jnp.bfloat16)
+    return jnp.dot(flags.astype(jnp.bfloat16), spread, preferred_element_type=jnp.float32)
+
+
+def build_bands(bank_ref, flag_ref, base_ref, band_ref, block_rows):
     out_count, edge, mid, edge_rows, mid_rows, total_rows, period = row_plan(block_rows)
-    flags = flag_ref[...].astype(jnp.float32)
+    filters = bank_ref.shape[1]
+    to_real, to_imag = spread_taps(bank_ref)
+    rest = jnp.zeros((filters, period - to_real.shape[1]), jnp.float32)
+    to_real = jnp.concatenate([to_real, rest], axis=1)
+    to_imag = pltpu.roll(jnp.concatenate([to_imag, rest], axis=1), period - AVG, 1)
+    is_real = lax.broadcasted_iota(jnp.int32, (8, period), 0) % 2 == 0
+    for f in range(filters):
+        rows = jnp.where(
+            is_real,
+            jnp.broadcast_to(to_real[f : f + 1], (8, period)),
+            jnp.broadcast_to(to_imag[f : f + 1], (8, period)),
+        )
+        base_ref[f] = pltpu.roll(rows, 0, 1, stride=AVG, stride_axis=0)
+    flags = spread_flags(flag_ref, block_rows)
     runs = ((-SIDE, edge, edge_rows), (out_count - SIDE, mid, mid_rows), (SIDE, edge, edge_rows))
+    lanes = round_up(2 * block_rows, 128) + 128
 
     def one_filter(f, carry):
-        base = jnp.concatenate([taps_ref[f]] * 4, axis=0)
-        tile = pltpu.roll(base, 0, 1, stride=AVG, stride_axis=0)
+        tile = base_ref[f]
         tiles = []
         for first, count, rows in runs:
             for row in range(0, rows, 8):
-                shift = (2 * AVG * first + AVG * row - 2 * HALF) % period
-                piece = pltpu.roll(tile, shift, 1)[:, : 2 * block_rows] * flags
+                start = (2 * HALF - 2 * AVG * first - AVG * row) % period
+                aligned = start // 128 * 128
+                piece = jnp.concatenate(
+                    [
+                        tile[:, at % period : at % period + 128]
+                        for at in range(aligned, aligned + lanes, 128)
+                    ],
+                    axis=1,
+                )
+                piece = pltpu.roll(piece, (aligned - start) % lanes, 1)[:, : 2 * block_rows]
+                piece = piece * flags
                 if row + 8 > 2 * count:
                     at = lax.broadcasted_iota(jnp.int32, piece.shape, 0)
                     piece = jnp.where(at < 2 * count - row, piece, 0.0)
@@ -70,24 +106,7 @@
         band_ref[f, total_rows:, :] = (band - high.astype(jnp.float32)).astype(jnp.bfloat16)
         return carry
 
-    lax.fori_loop(0, taps_ref.shape[0], one_filter, 0, unroll=4)
-
-
-def band_kernel(taps_ref, flag_ref, band_ref, *, block_rows):
-    build_bands(taps_ref, flag_ref, band_ref, block_rows)
-
-
-def band_call(taps, flags):
-    block_rows = flags.shape[1] // 2
-    total_rows = row_plan(block_rows)[5]
-    return pl.pallas_call(
-        functools.partial(band_kernel, block_rows=block_rows),
-        in_specs=[pl.BlockSpec(memory_space=pltpu.VMEM)] * 2,
-        out_specs=pl.BlockSpec(memory_space=pltpu.VMEM),
-        out_shape=jax.ShapeDtypeStruct(
-            (taps.shape[0], 2 * total_rows, 2 * block_rows), jnp.bfloat16
-        ),
-    )(taps, flags)
+    lax.fori_loop(0, filters, one_filter, 0, unroll=2)
 
 
 def encode(value, code_ref, step_ref, i):
@@ -105,9 +124,12 @@
 
 def stream_kernel(
     index_ref,
-    band_ref,
+    bank_ref,
+    flag_ref,
     vis_ref,
     out_ref,
+    base_ref,
+    band_ref,
     slab_ref,
     sum_ref,
     edge_ref,
@@ -254,6 +276,7 @@
             device_id={"tm": lax.rem(me + offset, count)},
             device_id_type=pl.DeviceIdType.MESH,
         )
+    build_bands(bank_ref, flag_ref, base_ref, band_ref, block_rows)
     pl.semaphore_wait(barrier, count - 1)
 
     def flow(owner):
@@ -455,10 +478,11 @@
     lax.fori_loop(0, count - 1, collect, 0)
 
 
-def stream_call(kernel_index, bands, visibilities):
+def stream_call(kernel_index, filter_bank, flags, visibilities):
     block_rows, bases, _, channels = visibilities.shape
     count = lax.axis_size("tm")
-    out_count, edge, mid, _, _, total_rows, _ = row_plan(block_rows)
+    out_count, edge, mid, _, _, total_rows, period = row_plan(block_rows)
+    filters = filter_bank.shape[1]
     owned = bases // count
     group = GROUP
     while owned % group:
@@ -471,11 +495,14 @@
         in_specs=[
             pl.BlockSpec(memory_space=pltpu.SMEM),
             pl.BlockSpec(memory_space=pltpu.VMEM),
+            pl.BlockSpec(memory_space=pltpu.VMEM),
             pl.BlockSpec(memory_space=pl.ANY),
         ],
         out_specs=pl.BlockSpec(memory_space=pl.ANY),
         out_shape=jax.ShapeDtypeStruct((count * out_count, owned, 2, channels), jnp.bfloat16),
         scratch_shapes=[
+            pltpu.VMEM((filters, 8, period), jnp.float32),
+            pltpu.VMEM((filters, 2 * total_rows, 2 * block_rows), jnp.bfloat16),
             pltpu.VMEM((LOADS, block_rows, group, 2, channels), jnp.bfloat16),
             pltpu.VMEM((chunks, group, total_rows, channels), jnp.float32),
             pltpu.VMEM((chunks, edge, group, 2, channels), jnp.int16),
@@ -501,17 +528,13 @@
             pltpu.SemaphoreType.DMA((parts,)),
         ],
         compiler_params=pltpu.CompilerParams(
-            collective_id=0, has_side_effects=True, vmem_limit_bytes=56 * 1024 * 1024
+            collective_id=0, has_side_effects=True, vmem_limit_bytes=40 * 1024 * 1024
         ),
-    )(kernel_index, bands, visibilities)
+    )(kernel_index, filter_bank, flags, visibilities)
 
 
 def per_device(visibilities, flag_mask, kernel_index, filter_bank):
-    period = row_plan(visibilities.shape[0])[6]
-    taps = averaged_taps(filter_bank, period)
-    flags = jnp.repeat(flag_mask, 2)[None, :]
-    bands = band_call(taps, flags)
-    return stream_call(kernel_index, bands, visibilities)
+    return stream_call(kernel_index, filter_bank, flag_mask[None, :], visibilities)
 
 
 def solution(mesh):

time: 79.3 us -> 67.5 us (0.85)
  Pallas kernels: 69.6 us -> 63.9 us
  local copies, waits for them, and re-layouts: 6.88 us -> 3.41 us
  other arithmetic: 2.43 us -> 0 us
    pallas_call x1 -> x0, Pallas kernels: 5.04 us -> none  [band_call(): pl.pallas_call(functools.partial(band_kernel, block_rows=block_rows), in_...]
    add x1 -> x0, other arithmetic: 1.55 us -> none  [averaged_taps(): total = total + padded[:, :, shift:shift + width]]
    another operation x5 -> x0, local copies, waits for them, and re-layouts: 1.24 us -> none  [the longest x1 0.74 us: per_device(): flags = jnp.repeat(flag_mask, 2)[None, :]]
    unnamed x1 -> x7, local copies, waits for them, and re-layouts: 4.17 us -> 3.41 us
where the time goes in v2:
time: 67.5 us; the launch traced here: 67.3 us
  Pallas kernels  63.9 us (95%)
  local copies, waits for them, and re-layouts  3.41 us (5%)
    pallas_call x1, Pallas kernels, stream_call(): pl.pallas_call(functools.partial(stream_kernel, count=count), in_specs=[p...  63.9 us
    unnamed x7, local copies, waits for them, and re-layouts  3.41 us

profile of v2, /device:TPU:8, one launch (start us, length us, event | category | flops | bytes accessed | tf_op | source)
XLA Modules:
  0.0 67.3 jit_solution(449285446885830061)
XLA Ops:
  0.0 0.0 copy-start
  0.0 0.8 %copy-done = f32[2,16,257]{2,1,0:T(8,128)S(1)} copy-done((f32[2,16,257]{2,1,0:T(8,128)S(1)}, f32[2,16,257]{2,1,0:T(8,128)}, u32[]{:S(2)}) %copy-start) | copy-done | bytes 32920
  0.8 0.0 copy-start.1
  0.8 0.7 %copy-done.1 = s32[200]{0:T(256)S(1)} copy-done((s32[200]{0:T(256)S(1)}, s32[200]{0:T(256)}, u32[]{:S(2)}) %copy-start.1) | copy-done | bytes 824
  1.5 0.0 copy-start.2
  1.5 0.7 copy-done.2
  2.1 63.9 %shard_map.46 = bf16[80,16,2,384]{3,2,1,0:T(2,128)(2,1)S(1)} custom-call(s32[64]{0:T(128)S(1)} %copy-done.2, f32[2,16,257]{2,1,0:T(8,128)S(1)} %copy-done, s32[1,200]{1,0:T(1,128)S(1)} %bitcast.1, bf16[200,64,2,384]{3,2,1,0:T(2,128)(2,1)} %vis_ref.1), custom_call_target="tpu_custom_call" | custom-call | tf_op jit(solution)/shard_map/pallas_call | solution.py:493
  66.1 1.3 %copy.6 = bf16[80,16,2,384]{3,2,1,0:T(2,128)(2,1)} copy(bf16[80,16,2,384]{3,2,1,0:T(2,128)(2,1)S(1)} %shard_map.46) | data formatting | bytes 3932160
Async XLA Ops:
  0.0 0.8 %copy-start = (f32[2,16,257]{2,1,0:T(8,128)S(1)}, f32[2,16,257]{2,1,0:T(8,128)}, u32[]{:S(2)}) copy-start(f32[2,16,257]{2,1,0:T(8,128)} %bank_ref.1) | copy-start | bytes 98692
  0.8 0.7 %copy-start.1 = (s32[200]{0:T(256)S(1)}, s32[200]{0:T(256)}, u32[]{:S(2)}) copy-start(s32[200]{0:T(256)} %param.5) | copy-start | bytes 2404
  1.5 0.7 copy-start.2

commit v3 on v2

--- a/solution.py
+++ b/solution.py
@@ -33,18 +33,21 @@
     return out_count, edge, mid, edge_rows, mid_rows, total_rows, period
 
 
-def spread_taps(bank_ref):
-    filters, taps = bank_ref.shape[1:]
+def tap_spread(taps):
     width = round_up(2 * (taps + AVG), 128)
+    ahead = lax.broadcasted_iota(jnp.int32, (taps, width), 1)
+    ahead = ahead - 2 * lax.broadcasted_iota(jnp.int32, (taps, width), 0)
+    hit = jnp.logical_and(jnp.logical_and(ahead >= 0, ahead < 2 * AVG), ahead % 2 == 0)
+    return jnp.where(hit, 1.0, 0.0).astype(jnp.bfloat16)
+
+
+def spread_taps(bank_ref, spread):
+    filters = bank_ref.shape[1]
     parts = []
     for part in (bank_ref[0], bank_ref[1]):
         for _ in range(3):
             parts.append(part.astype(jnp.bfloat16))
             part = part - parts[-1].astype(jnp.float32)
-    ahead = lax.broadcasted_iota(jnp.int32, (taps, width), 1)
-    ahead = ahead - 2 * lax.broadcasted_iota(jnp.int32, (taps, width), 0)
-    hit = jnp.logical_and(jnp.logical_and(ahead >= 0, ahead < 2 * AVG), ahead % 2 == 0)
-    spread = jnp.where(hit, 1.0, 0.0).astype(jnp.bfloat16)
     total = jnp.dot(jnp.concatenate(parts, axis=0), spread, preferred_element_type=jnp.float32)
     total = [total[filters * k : filters * (k + 1)] for k in range(6)]
     real = (total[0] + total[1] + total[2]) * (1.0 / AVG)
@@ -52,19 +55,25 @@
     return real - pltpu.roll(imag, 1, 1), imag + pltpu.roll(real, 1, 1)
 
 
-def spread_flags(flag_ref, block_rows):
-    flags = jnp.broadcast_to(flag_ref[...], (8, block_rows)).astype(jnp.float32)
+def flag_spread(block_rows):
     ahead = lax.broadcasted_iota(jnp.int32, (block_rows, 2 * block_rows), 1)
     ahead = ahead - 2 * lax.broadcasted_iota(jnp.int32, (block_rows, 2 * block_rows), 0)
     hit = jnp.logical_and(ahead >= 0, ahead < 2)
-    spread = jnp.where(hit, 1.0, 0.0).astype(jnp.bfloat16)
+    return jnp.where(hit, 1.0, 0.0).astype(jnp.bfloat16)
+
+
+def spread_flags(flag_ref, spread):
+    flags = jnp.broadcast_to(flag_ref[...], (8, flag_ref.shape[1])).astype(jnp.float32)
     return jnp.dot(flags.astype(jnp.bfloat16), spread, preferred_element_type=jnp.float32)
 
 
-def build_bands(bank_ref, flag_ref, base_ref, band_ref, block_rows):
+def build_bands(bank_ref, flag_ref, base_ref, band_ref, block_rows, copies):
     out_count, edge, mid, edge_rows, mid_rows, total_rows, period = row_plan(block_rows)
     filters = bank_ref.shape[1]
-    to_real, to_imag = spread_taps(bank_ref)
+    tap_matrix, flag_matrix = tap_spread(bank_ref.shape[2]), flag_spread(block_rows)
+    for copy in copies:
+        copy.wait()
+    to_real, to_imag = spread_taps(bank_ref, tap_matrix)
     rest = jnp.zeros((filters, period - to_real.shape[1]), jnp.float32)
     to_real = jnp.concatenate([to_real, rest], axis=1)
     to_imag = pltpu.roll(jnp.concatenate([to_imag, rest], axis=1), period - AVG, 1)
@@ -76,7 +85,7 @@
             jnp.broadcast_to(to_imag[f : f + 1], (8, period)),
         )
         base_ref[f] = pltpu.roll(rows, 0, 1, stride=AVG, stride_axis=0)
-    flags = spread_flags(flag_ref, block_rows)
+    flags = spread_flags(flag_ref, flag_matrix)
     runs = ((-SIDE, edge, edge_rows), (out_count - SIDE, mid, mid_rows), (SIDE, edge, edge_rows))
     lanes = round_up(2 * block_rows, 128) + 128
 
@@ -109,12 +118,16 @@
     lax.fori_loop(0, filters, one_filter, 0, unroll=2)
 
 
-def encode(value, code_ref, step_ref, i):
-    peak = jnp.max(jnp.max(jnp.abs(value), axis=0, keepdims=True), axis=1, keepdims=True)
-    peak = jnp.maximum(peak, TINY)
-    step_ref[i : i + 1, :] = jnp.broadcast_to(peak * (1.0 / LEVELS), (1, step_ref.shape[1]))
-    code = jnp.round(value * (LEVELS / peak)).astype(jnp.int32).astype(jnp.int16)
-    code_ref[:, i] = code.reshape(-1, 2, value.shape[1])
+def encode(values, code_ref, step_ref):
+    lane = lax.broadcasted_iota(jnp.int32, (1, 128), 1)
+    steps = jnp.zeros((1, 128), jnp.float32)
+    for i, value in enumerate(values):
+        peak = jnp.max(jnp.max(jnp.abs(value), axis=0, keepdims=True), axis=1, keepdims=True)
+        peak = jnp.maximum(peak, TINY)
+        steps = jnp.where(lane == i, peak * (1.0 / LEVELS), steps)
+        code = jnp.round(value * (LEVELS / peak)).astype(jnp.int32).astype(jnp.int16)
+        code_ref[:, i] = code.reshape(-1, 2, value.shape[1])
+    step_ref[...] = steps
 
 
 def decode(code):
@@ -123,11 +136,14 @@
 
 
 def stream_kernel(
+    index_hbm,
+    bank_hbm,
+    flag_hbm,
+    vis_ref,
+    out_ref,
     index_ref,
     bank_ref,
     flag_ref,
-    vis_ref,
-    out_ref,
     base_ref,
     band_ref,
     slab_ref,
@@ -141,6 +157,7 @@
     in_mid_step_ref,
     done_ref,
     own_ref,
+    small_sem,
     load_sem,
     edge_send,
     edge_step_send,
@@ -266,6 +283,14 @@
             own_sem.at[part],
         )
 
+    smalls = [
+        pltpu.make_async_copy(source, target, small_sem.at[k])
+        for k, (source, target) in enumerate(
+            ((bank_hbm, bank_ref), (flag_hbm, flag_ref), (index_hbm, index_ref))
+        )
+    ]
+    for copy in smalls:
+        copy.start()
     for step in range(LOADS - 1):
         load(step).start()
     barrier = pltpu.get_barrier_semaphore()
@@ -276,7 +301,7 @@
             device_id={"tm": lax.rem(me + offset, count)},
             device_id_type=pl.DeviceIdType.MESH,
         )
-    build_bands(bank_ref, flag_ref, base_ref, band_ref, block_rows)
+    build_bands(bank_ref, flag_ref, base_ref, band_ref, block_rows, smalls)
     pl.semaphore_wait(barrier, count - 1)
 
     def flow(owner):
@@ -303,78 +328,103 @@
         @pl.when(owner != me)
         def _():
             start = pl.multiple_of(jnp.where(rightward, far_at, 0), 8)
-            for i in range(group):
-                encode(
-                    sum_ref[chunk, i, pl.ds(start, 2 * edge), :],
-                    edge_ref.at[chunk],
-                    edge_step_ref.at[chunk],
-                    i,
-                )
+            values = [sum_ref[chunk, i, pl.ds(start, 2 * edge), :] for i in range(group)]
+            encode(values, edge_ref.at[chunk], edge_step_ref.at[chunk])
             for copy in edge_copies(chunk, landing, rightward, target):
                 copy.start()
 
-        @pl.when(jnp.logical_and(owner != me, jnp.logical_not(upstream)))
-        def _():
-            for i in range(group):
-                encode(
-                    sum_ref[chunk, i, mid_at : mid_at + 2 * mid, :],
-                    mid_ref.at[chunk],
-                    mid_step_ref.at[chunk],
-                    i,
-                )
-            for copy in mid_copies(chunk, landing, rightward, target):
-                copy.start()
+        ends = jnp.logical_and(owner != me, jnp.logical_not(upstream))
+
+        @pl.when(ends)
+        def _():
+            values = [sum_ref[chunk, i, mid_at : mid_at + 2 * mid, :] for i in range(group)]
+            encode(values, mid_ref.at[chunk], mid_step_ref.at[chunk])
+
+        turn = step // per_owner
+        paired = jnp.logical_or(turn % 2 == 1, turn == count - 2)
+        paired = jnp.logical_and(paired, part == per_owner - 1)
+
+        @pl.when(jnp.logical_and(ends, paired))
+        def _():
+            def start_mid(back, carry):
+                owner, part, chunk = chunk_at(back)
+                rightward, _, target = flow(owner)
+                landing = slot_of(owner, part, chunk, target, rightward)
+                for copy in mid_copies(chunk, landing, rightward, target):
+                    copy.start()
+                return carry
+
+            lax.fori_loop((turn - turn % 2) * per_owner, step + 1, start_mid, 0)
 
         return carry
 
     lax.fori_loop(0, chunks, compute, 0)
-
-    def step_of(step_ref, slot, i):
-        return jnp.concatenate([step_ref[slot, i : i + 1, :]] * (channels // 128), axis=1)
-
-    def finish(step, carry):
+    forward = chunks - per_owner
+
+    def came(slot, start, rows, i):
+        return decode(in_ref[slot, pl.ds(start, rows), i])
+
+    def pass_mid(step, carry):
         owner, part, chunk = chunk_at(step)
         rightward, upstream, target = flow(owner)
         landing = slot_of(owner, part, chunk, target, rightward)
-        forward = owner != me
-
-        @pl.when(jnp.logical_and(forward, upstream))
+
+        @pl.when(upstream)
         def _():
             for copy in edge_copies(chunk, chunk, rightward, target):
                 copy.wait_recv()
             start = jnp.where(rightward, edge, 0)
-            for i in range(group):
-                came = decode(in_ref[chunk, pl.ds(start, mid), i])
-                value = sum_ref[chunk, i, mid_at : mid_at + 2 * mid, :]
-                value = value + came * step_of(in_edge_step_ref, chunk, i)
-                encode(value, mid_ref.at[chunk], mid_step_ref.at[chunk], i)
+            units = in_edge_step_ref[chunk]
+            values = [
+                sum_ref[chunk, i, mid_at : mid_at + 2 * mid, :]
+                + came(chunk, start, mid, i) * units[:, i : i + 1]
+                for i in range(group)
+            ]
+            encode(values, mid_ref.at[chunk], mid_step_ref.at[chunk])
             for copy in mid_copies(chunk, landing, rightward, target):
                 copy.start()
+
+        return carry
+
+    lax.fori_loop(0, forward, pass_mid, 0)
+
+    def round_off(value, rows):
+        return value.astype(jnp.bfloat16).reshape(rows, 2, channels)
+
+    def pass_done(step, carry):
+        owner, part, chunk = chunk_at(step)
+        rightward, upstream, target = flow(owner)
+        near = pl.multiple_of(jnp.where(rightward, 0, far_at), 8)
+
+        @pl.when(upstream)
+        def _():
             for copy in mid_copies(chunk, chunk, rightward, target):
                 copy.wait_recv()
             start = jnp.where(rightward, 0, mid)
-            near = pl.multiple_of(jnp.where(rightward, 0, far_at), 8)
             at = lax.broadcasted_iota(jnp.int32, (2 * edge, channels), 0)
             first = jnp.where(rightward, 0, 2 * (edge - mid))
             of_mid = jnp.logical_and(at >= first, at < first + 2 * mid)
+            mids, edges = in_mid_step_ref[chunk], in_edge_step_ref[chunk]
             for i in range(group):
-                came = decode(in_ref[chunk, pl.ds(start, edge), i])
-                unit = jnp.where(
-                    of_mid,
-                    step_of(in_mid_step_ref, chunk, i),
-                    step_of(in_edge_step_ref, chunk, i),
-                )
-                value = sum_ref[chunk, i, pl.ds(near, 2 * edge), :] + came * unit
-                done_ref[chunk, :, i] = value.astype(jnp.bfloat16).reshape(edge, 2, channels)
+                unit = jnp.where(of_mid, mids[:, i : i + 1], edges[:, i : i + 1])
+                value = sum_ref[chunk, i, pl.ds(near, 2 * edge), :]
+                value = value + came(chunk, start, edge, i) * unit
+                done_ref[chunk, :, i] = round_off(value, edge)
             full_done(me, chunk, part, rightward, owner).start()
 
-        @pl.when(jnp.logical_and(forward, jnp.logical_not(upstream)))
-        def _():
-            near = pl.multiple_of(jnp.where(rightward, 0, far_at), 8)
+        @pl.when(jnp.logical_not(upstream))
+        def _():
             for i in range(group):
                 value = sum_ref[chunk, i, pl.ds(near, 2 * edge), :]
-                done_ref[chunk, :, i] = value.astype(jnp.bfloat16).reshape(edge, 2, channels)
+                done_ref[chunk, :, i] = round_off(value, edge)
             short_done(me, chunk, part, rightward, owner).start()
+
+        return carry
+
+    lax.fori_loop(0, forward, pass_done, 0)
+
+    def pass_own(part, carry):
+        chunk = me * per_owner + part
 
         def from_side(slot, rightward, near, edge_start, first):
             for copy in edge_copies(chunk, slot, rightward, me):
@@ -383,49 +433,49 @@
                 copy.wait_recv()
             at = lax.broadcasted_iota(jnp.int32, (2 * edge, channels), 0)
             of_mid = jnp.logical_and(at >= first, at < first + 2 * mid)
+            mids, edges = in_mid_step_ref[slot], in_edge_step_ref[slot]
+            start = edge if rightward else 0
             for i in range(group):
-                edge_unit = step_of(in_edge_step_ref, slot, i)
-                unit = jnp.where(of_mid, step_of(in_mid_step_ref, slot, i), edge_unit)
-                came = decode(in_ref[slot, edge_start : edge_start + edge, i])
-                sum_ref[chunk, i, near : near + 2 * edge, :] += came * unit
-                start = edge if rightward else 0
-                came = decode(in_ref[slot, start : start + mid, i])
-                sum_ref[chunk, i, mid_at : mid_at + 2 * mid, :] += came * edge_unit
-
-        @pl.when(jnp.logical_and(owner == me, has_left))
+                unit = jnp.where(of_mid, mids[:, i : i + 1], edges[:, i : i + 1])
+                sum_ref[chunk, i, near : near + 2 * edge, :] += (
+                    came(slot, edge_start, edge, i) * unit
+                )
+                sum_ref[chunk, i, mid_at : mid_at + 2 * mid, :] += (
+                    came(slot, start, mid, i) * edges[:, i : i + 1]
+                )
+
+        @pl.when(has_left)
         def _():
             from_side(chunk, True, 0, 0, 0)
 
-        @pl.when(jnp.logical_and(owner == me, has_right))
+        @pl.when(has_right)
         def _():
             from_side(chunks + part, False, far_at, mid, 2 * (edge - mid))
 
-        @pl.when(owner == me)
-        def _():
-            for i in range(group):
-                for row, rows, start in (
-                    (0, edge, 0),
-                    (edge, mid, mid_at),
-                    (edge + mid, edge, far_at),
-                ):
-                    value = sum_ref[chunk, i, start : start + 2 * rows, :].astype(jnp.bfloat16)
-                    own_ref[part, row : row + rows, i] = value.reshape(rows, 2, channels)
-
-            @pl.when(jnp.logical_and(has_left, has_right))
-            def _():
-                keep(part, 0, 2 * edge + mid).start()
-
-            @pl.when(jnp.logical_not(has_left))
-            def _():
-                keep(part, SIDE, out_count + SIDE).start()
-
-            @pl.when(jnp.logical_not(has_right))
-            def _():
-                keep(part, 0, out_count + SIDE).start()
+        for i in range(group):
+            for row, rows, start in (
+                (0, edge, 0),
+                (edge, mid, mid_at),
+                (edge + mid, edge, far_at),
+            ):
+                value = sum_ref[chunk, i, start : start + 2 * rows, :]
+                own_ref[part, row : row + rows, i] = round_off(value, rows)
+
+        @pl.when(jnp.logical_and(has_left, has_right))
+        def _():
+            keep(part, 0, 2 * edge + mid).start()
+
+        @pl.when(jnp.logical_not(has_left))
+        def _():
+            keep(part, SIDE, out_count + SIDE).start()
+
+        @pl.when(jnp.logical_not(has_right))
+        def _():
+            keep(part, 0, out_count + SIDE).start()
 
         return carry
 
-    lax.fori_loop(0, chunks, finish, 0)
+    lax.fori_loop(0, per_owner, pass_own, 0)
 
     def drain(step, carry):
         owner, part, chunk = chunk_at(step)
@@ -489,31 +539,39 @@
         group //= 2
     chunks, parts = bases // group, owned // group
     slots = chunks + parts
+    small = [
+        pltpu.with_memory_space_constraint(operand, pltpu.HBM)
+        for operand in (kernel_index, filter_bank, flags)
+    ]
     sent, landed = pltpu.SemaphoreType.DMA((chunks,)), pltpu.SemaphoreType.DMA((slots,))
     return pl.pallas_call(
         functools.partial(stream_kernel, count=count),
         in_specs=[
-            pl.BlockSpec(memory_space=pltpu.SMEM),
-            pl.BlockSpec(memory_space=pltpu.VMEM),
-            pl.BlockSpec(memory_space=pltpu.VMEM),
+            pl.BlockSpec(memory_space=pltpu.HBM),
+            pl.BlockSpec(memory_space=pltpu.HBM),
+            pl.BlockSpec(memory_space=pltpu.HBM),
             pl.BlockSpec(memory_space=pl.ANY),
         ],
         out_specs=pl.BlockSpec(memory_space=pl.ANY),
         out_shape=jax.ShapeDtypeStruct((count * out_count, owned, 2, channels), jnp.bfloat16),
         scratch_shapes=[
+            pltpu.SMEM(kernel_index.shape, jnp.int32),
+            pltpu.VMEM(filter_bank.shape, jnp.float32),
+            pltpu.VMEM(flags.shape, jnp.int32),
             pltpu.VMEM((filters, 8, period), jnp.float32),
             pltpu.VMEM((filters, 2 * total_rows, 2 * block_rows), jnp.bfloat16),
             pltpu.VMEM((LOADS, block_rows, group, 2, channels), jnp.bfloat16),
             pltpu.VMEM((chunks, group, total_rows, channels), jnp.float32),
             pltpu.VMEM((chunks, edge, group, 2, channels), jnp.int16),
-            pltpu.VMEM((chunks, group, 128), jnp.float32),
+            pltpu.VMEM((chunks, 1, 128), jnp.float32),
             pltpu.VMEM((chunks, mid, group, 2, channels), jnp.int16),
-            pltpu.VMEM((chunks, group, 128), jnp.float32),
+            pltpu.VMEM((chunks, 1, 128), jnp.float32),
             pltpu.VMEM((slots, edge + mid, group, 2, channels), jnp.int16),
-            pltpu.VMEM((slots, group, 128), jnp.float32),
-            pltpu.VMEM((slots, group, 128), jnp.float32),
+            pltpu.VMEM((slots, 1, 128), jnp.float32),
+            pltpu.VMEM((slots, 1, 128), jnp.float32),
             pltpu.VMEM((chunks, edge, group, 2, channels), jnp.bfloat16),
             pltpu.VMEM((parts, 2 * edge + mid, group, 2, channels), jnp.bfloat16),
+            pltpu.SemaphoreType.DMA((3,)),
             pltpu.SemaphoreType.DMA((LOADS,)),
             sent,
             sent,
@@ -530,7 +588,7 @@
         compiler_params=pltpu.CompilerParams(
             collective_id=0, has_side_effects=True, vmem_limit_bytes=40 * 1024 * 1024
         ),
-    )(kernel_index, filter_bank, flags, visibilities)
+    )(*small, visibilities)
 
 
 def per_device(visibilities, flag_mask, kernel_index, filter_bank):

time: 67.5 us -> 64.7 us (0.959)
  local copies, waits for them, and re-layouts: 3.41 us -> 1.27 us
    unnamed x7 -> x1, local copies, waits for them, and re-layouts: 3.41 us -> 1.27 us
where the time goes in v3:
time: 64.7 us; the launch traced here: 64.6 us
  Pallas kernels  63.3 us (98%)
  local copies, waits for them, and re-layouts  1.27 us (2%)
    pallas_call x1, Pallas kernels, stream_call(): pl.pallas_call(functools.partial(stream_kernel, count=count), in_specs=[p...  63.3 us

profile of v3, /device:TPU:8, one launch (start us, length us, event | category | flops | bytes accessed | tf_op | source)
XLA Modules:
  0.0 64.6 jit_solution(7807069958770586633)
XLA Ops:
  0.0 63.3 %shard_map.46 = bf16[80,16,2,384]{3,2,1,0:T(2,128)(2,1)S(1)} custom-call(s32[64]{0:T(128)} %index_hbm.1, f32[2,16,257]{2,1,0:T(8,128)} %bank_hbm.1, s32[1,200]{1,0:T(1,128)} %bitcast.1, bf16[200,64,2,384]{3,2,1,0:T(2,128)(2,1)} %vis_ref.1), custom_call_target="tpu_custom_call" | custom-call | tf_op jit(solution)/shard_map/pallas_call | solution.py:547
  63.3 1.3 %copy.6 = bf16[80,16,2,384]{3,2,1,0:T(2,128)(2,1)} copy(bf16[80,16,2,384]{3,2,1,0:T(2,128)(2,1)S(1)} %shard_map.46) | data formatting | bytes 3932160

commit v4 on v3

--- a/solution.py
+++ b/solution.py
@@ -67,55 +67,49 @@
     return jnp.dot(flags.astype(jnp.bfloat16), spread, preferred_element_type=jnp.float32)
 
 
-def build_bands(bank_ref, flag_ref, base_ref, band_ref, block_rows, copies):
-    out_count, edge, mid, edge_rows, mid_rows, total_rows, period = row_plan(block_rows)
-    filters = bank_ref.shape[1]
+def build_rows(bank_ref, flag_ref, real_ref, imag_ref, good_ref, block_rows, copies):
+    period = row_plan(block_rows)[6]
     tap_matrix, flag_matrix = tap_spread(bank_ref.shape[2]), flag_spread(block_rows)
     for copy in copies:
         copy.wait()
     to_real, to_imag = spread_taps(bank_ref, tap_matrix)
-    rest = jnp.zeros((filters, period - to_real.shape[1]), jnp.float32)
-    to_real = jnp.concatenate([to_real, rest], axis=1)
-    to_imag = pltpu.roll(jnp.concatenate([to_imag, rest], axis=1), period - AVG, 1)
+    rest = jnp.zeros((to_real.shape[0], period - to_real.shape[1]), jnp.float32)
+    real_ref[...] = jnp.concatenate([to_real, rest], axis=1)
+    imag_ref[...] = pltpu.roll(jnp.concatenate([to_imag, rest], axis=1), period - AVG, 1)
+    good_ref[...] = spread_flags(flag_ref, flag_matrix)
+
+
+def build_band(real, imag, flags, block_rows):
+    out_count, edge, mid, edge_rows, mid_rows, total_rows, period = row_plan(block_rows)
     is_real = lax.broadcasted_iota(jnp.int32, (8, period), 0) % 2 == 0
-    for f in range(filters):
-        rows = jnp.where(
-            is_real,
-            jnp.broadcast_to(to_real[f : f + 1], (8, period)),
-            jnp.broadcast_to(to_imag[f : f + 1], (8, period)),
-        )
-        base_ref[f] = pltpu.roll(rows, 0, 1, stride=AVG, stride_axis=0)
-    flags = spread_flags(flag_ref, flag_matrix)
+    tile = jnp.where(
+        is_real, jnp.broadcast_to(real, (8, period)), jnp.broadcast_to(imag, (8, period))
+    )
+    tile = pltpu.roll(tile, 0, 1, stride=AVG, stride_axis=0)
     runs = ((-SIDE, edge, edge_rows), (out_count - SIDE, mid, mid_rows), (SIDE, edge, edge_rows))
     lanes = round_up(2 * block_rows, 128) + 128
-
-    def one_filter(f, carry):
-        tile = base_ref[f]
-        tiles = []
-        for first, count, rows in runs:
-            for row in range(0, rows, 8):
-                start = (2 * HALF - 2 * AVG * first - AVG * row) % period
-                aligned = start // 128 * 128
-                piece = jnp.concatenate(
-                    [
-                        tile[:, at % period : at % period + 128]
-                        for at in range(aligned, aligned + lanes, 128)
-                    ],
-                    axis=1,
-                )
-                piece = pltpu.roll(piece, (aligned - start) % lanes, 1)[:, : 2 * block_rows]
-                piece = piece * flags
-                if row + 8 > 2 * count:
-                    at = lax.broadcasted_iota(jnp.int32, piece.shape, 0)
-                    piece = jnp.where(at < 2 * count - row, piece, 0.0)
-                tiles.append(piece)
-        band = jnp.concatenate(tiles, axis=0)
-        high = band.astype(jnp.bfloat16)
-        band_ref[f, :total_rows, :] = high
-        band_ref[f, total_rows:, :] = (band - high.astype(jnp.float32)).astype(jnp.bfloat16)
-        return carry
-
-    lax.fori_loop(0, filters, one_filter, 0, unroll=2)
+    tiles = []
+    for first, count, rows in runs:
+        for row in range(0, rows, 8):
+            start = (2 * HALF - 2 * AVG * first - AVG * row) % period
+            aligned = start // 128 * 128
+            piece = jnp.concatenate(
+                [
+                    tile[:, at % period : at % period + 128]
+                    for at in range(aligned, aligned + lanes, 128)
+                ],
+                axis=1,
+            )
+            piece = pltpu.roll(piece, (aligned - start) % lanes, 1)[:, : 2 * block_rows]
+            piece = piece * flags
+            if row + 8 > 2 * count:
+                at = lax.broadcasted_iota(jnp.int32, piece.shape, 0)
+                piece = jnp.where(at < 2 * count - row, piece, 0.0)
+            tiles.append(piece)
+    band = jnp.concatenate(tiles, axis=0)
+    high = band.astype(jnp.bfloat16)
+    low = (band - high.astype(jnp.float32)).astype(jnp.bfloat16)
+    return jnp.concatenate([high, low], axis=0)
 
 
 def encode(values, code_ref, step_ref):
@@ -144,8 +138,9 @@
     index_ref,
     bank_ref,
     flag_ref,
-    base_ref,
-    band_ref,
+    real_ref,
+    imag_ref,
+    good_ref,
     slab_ref,
     sum_ref,
     edge_ref,
@@ -193,11 +188,16 @@
         )
         return owner, part, owner * per_owner + part
 
-    def load(step):
+    pieces = load_sem.shape[1]
+    share = group // pieces
+
+    def load(step, piece):
         _, _, chunk = chunk_at(step)
         slot = step % LOADS
         return pltpu.make_async_copy(
-            vis_ref.at[:, pl.ds(chunk * group, group)], slab_ref.at[slot], load_sem.at[slot]
+            vis_ref.at[:, pl.ds(chunk * group + piece * share, share)],
+            slab_ref.at[slot, :, pl.ds(piece * share, share)],
+            load_sem.at[slot, piece],
         )
 
     def remote(source, target, send_sem, recv_sem, device):
@@ -291,8 +291,8 @@
     ]
     for copy in smalls:
         copy.start()
-    for step in range(LOADS - 1):
-        load(step).start()
+    for piece in range(pieces):
+        load(0, piece).start()
     barrier = pltpu.get_barrier_semaphore()
     for offset in range(1, count):
         pl.semaphore_signal(
@@ -301,7 +301,10 @@
             device_id={"tm": lax.rem(me + offset, count)},
             device_id_type=pl.DeviceIdType.MESH,
         )
-    build_bands(bank_ref, flag_ref, base_ref, band_ref, block_rows, smalls)
+    build_rows(bank_ref, flag_ref, real_ref, imag_ref, good_ref, block_rows, smalls)
+    for step in range(1, LOADS - 1):
+        for piece in range(pieces):
+            load(step, piece).start()
     pl.semaphore_wait(barrier, count - 1)
 
     def flow(owner):
@@ -312,17 +315,21 @@
     def compute(step, carry):
         @pl.when(step + LOADS - 1 < chunks)
         def _():
-            load(step + LOADS - 1).start()
-
-        load(step).wait()
+            for piece in range(pieces):
+                load(step + LOADS - 1, piece).start()
+
         owner, part, chunk = chunk_at(step)
         slot = step % LOADS
         rightward, upstream, target = flow(owner)
         landing = slot_of(owner, part, chunk, target, rightward)
         for i in range(group):
+            if i % share == 0:
+                load(step, i // share).wait()
             which = index_ref[chunk * group + i]
+            real, imag = real_ref[pl.ds(which, 1), :], imag_ref[pl.ds(which, 1), :]
+            band = build_band(real, imag, good_ref[...], block_rows)
             slab = slab_ref[slot, :, i].reshape(2 * block_rows, channels)
-            both = jnp.dot(band_ref[which], slab, preferred_element_type=jnp.float32)
+            both = jnp.dot(band, slab, preferred_element_type=jnp.float32)
             sum_ref[chunk, i] = both[:total_rows] + both[total_rows:]
 
         @pl.when(owner != me)
@@ -558,8 +565,9 @@
             pltpu.SMEM(kernel_index.shape, jnp.int32),
             pltpu.VMEM(filter_bank.shape, jnp.float32),
             pltpu.VMEM(flags.shape, jnp.int32),
-            pltpu.VMEM((filters, 8, period), jnp.float32),
-            pltpu.VMEM((filters, 2 * total_rows, 2 * block_rows), jnp.bfloat16),
+            pltpu.VMEM((filters, period), jnp.float32),
+            pltpu.VMEM((filters, period), jnp.float32),
+            pltpu.VMEM((8, 2 * block_rows), jnp.float32),
             pltpu.VMEM((LOADS, block_rows, group, 2, channels), jnp.bfloat16),
             pltpu.VMEM((chunks, group, total_rows, channels), jnp.float32),
             pltpu.VMEM((chunks, edge, group, 2, channels), jnp.int16),
@@ -572,7 +580,7 @@
             pltpu.VMEM((chunks, edge, group, 2, channels), jnp.bfloat16),
             pltpu.VMEM((parts, 2 * edge + mid, group, 2, channels), jnp.bfloat16),
             pltpu.SemaphoreType.DMA((3,)),
-            pltpu.SemaphoreType.DMA((LOADS,)),
+            pltpu.SemaphoreType.DMA((LOADS, 2 if group % 2 == 0 else 1)),
             sent,
             sent,
             sent,

time: 64.7 us -> 63.8 us (0.986)
  Pallas kernels: 63.3 us -> 62.4 us
    pallas_call x1, Pallas kernels: 63.3 us -> 62.4 us  [stream_call(): pl.pallas_call(functools.partial(stream_kernel, count=count), in_specs=[p...]
where the time goes in v4:
time: 63.8 us; the launch traced here: 63.7 us
  Pallas kernels  62.4 us (98%)
  local copies, waits for them, and re-layouts  1.27 us (2%)
    pallas_call x1, Pallas kernels, stream_call(): pl.pallas_call(functools.partial(stream_kernel, count=count), in_specs=[p...  62.4 us

profile of v4, /device:TPU:8, one launch (start us, length us, event | category | flops | bytes accessed | tf_op | source)
XLA Modules:
  0.0 63.7 jit_solution(6449546228177117742)
XLA Ops:
  0.0 62.4 %shard_map.46 = bf16[80,16,2,384]{3,2,1,0:T(2,128)(2,1)S(1)} custom-call(s32[64]{0:T(128)} %index_hbm.1, f32[2,16,257]{2,1,0:T(8,128)} %bank_hbm.1, s32[1,200]{1,0:T(1,128)} %bitcast.1, bf16[200,64,2,384]{3,2,1,0:T(2,128)(2,1)} %vis_ref.1), custom_call_target="tpu_custom_call" | custom-call | tf_op jit(solution)/shard_map/pallas_call | solution.py:554
  62.4 1.3 %copy.6 = bf16[80,16,2,384]{3,2,1,0:T(2,128)(2,1)} copy(bf16[80,16,2,384]{3,2,1,0:T(2,128)(2,1)S(1)} %shard_map.46) | data formatting | bytes 3932160

commit v5 on v4

--- a/solution.py
+++ b/solution.py
@@ -12,6 +12,7 @@
 HALF = TAPS // 2
 SIDE = -(-HALF // AVG)
 GROUP = 8
+PIECES = 2
 LOADS = 3
 LEVELS = 32767.0
 TINY = 1e-33
@@ -112,7 +113,7 @@
     return jnp.concatenate([high, low], axis=0)
 
 
-def encode(values, code_ref, step_ref):
+def encode(values, code_ref, step_ref, first=0):
     lane = lax.broadcasted_iota(jnp.int32, (1, 128), 1)
     steps = jnp.zeros((1, 128), jnp.float32)
     for i, value in enumerate(values):
@@ -120,7 +121,7 @@
         peak = jnp.maximum(peak, TINY)
         steps = jnp.where(lane == i, peak * (1.0 / LEVELS), steps)
         code = jnp.round(value * (LEVELS / peak)).astype(jnp.int32).astype(jnp.int16)
-        code_ref[:, i] = code.reshape(-1, 2, value.shape[1])
+        code_ref[:, first + i] = code.reshape(-1, 2, value.shape[1])
     step_ref[...] = steps
 
 
@@ -165,6 +166,8 @@
     done_send,
     done_recv,
     own_sem,
+    lefts_in,
+    rights_in,
     *,
     count,
 ):
@@ -214,24 +217,29 @@
         second = jnp.logical_and(owner == receiver, jnp.logical_not(rightward))
         return jnp.where(second, chunks + part, chunk)
 
+    def edge_copy(chunk, slot, rightward, device, piece):
+        start = jnp.where(rightward, mid, 0)
+        lot = pl.ds(piece * share, share)
+        return remote(
+            edge_ref.at[chunk, :, lot],
+            in_ref.at[slot, pl.ds(start, edge), lot],
+            edge_send.at[chunk, piece],
+            edge_recv.at[slot, piece],
+            device,
+        )
+
+    def edge_step_copy(chunk, slot, device):
+        return remote(
+            edge_step_ref.at[chunk],
+            in_edge_step_ref.at[slot],
+            edge_step_send.at[chunk],
+            edge_step_recv.at[slot],
+            device,
+        )
+
     def edge_copies(chunk, slot, rightward, device):
-        start = jnp.where(rightward, mid, 0)
-        return (
-            remote(
-                edge_ref.at[chunk],
-                in_ref.at[slot, pl.ds(start, edge)],
-                edge_send.at[chunk],
-                edge_recv.at[slot],
-                device,
-            ),
-            remote(
-                edge_step_ref.at[chunk],
-                in_edge_step_ref.at[slot],
-                edge_step_send.at[chunk],
-                edge_step_recv.at[slot],
-                device,
-            ),
-        )
+        copies = [edge_copy(chunk, slot, rightward, device, piece) for piece in range(pieces)]
+        return copies + [edge_step_copy(chunk, slot, device)]
 
     def mid_copies(chunk, slot, rightward, device):
         start = jnp.where(rightward, 0, edge)
@@ -293,19 +301,26 @@
         copy.start()
     for piece in range(pieces):
         load(0, piece).start()
+    def signal(semaphore, device):
+        pl.semaphore_signal(
+            semaphore, inc=1, device_id={"tm": device}, device_id_type=pl.DeviceIdType.MESH
+        )
+
     barrier = pltpu.get_barrier_semaphore()
-    for offset in range(1, count):
-        pl.semaphore_signal(
-            barrier,
-            inc=1,
-            device_id={"tm": lax.rem(me + offset, count)},
-            device_id_type=pl.DeviceIdType.MESH,
-        )
+
+    @pl.when(has_left)
+    def _():
+        signal(barrier, me - 1)
+
+    @pl.when(has_right)
+    def _():
+        signal(barrier, me + 1)
+
     build_rows(bank_ref, flag_ref, real_ref, imag_ref, good_ref, block_rows, smalls)
     for step in range(1, LOADS - 1):
         for piece in range(pieces):
             load(step, piece).start()
-    pl.semaphore_wait(barrier, count - 1)
+    pl.semaphore_wait(barrier, has_left.astype(jnp.int32) + has_right.astype(jnp.int32))
 
     def flow(owner):
         rightward = owner > me
@@ -322,23 +337,27 @@
         slot = step % LOADS
         rightward, upstream, target = flow(owner)
         landing = slot_of(owner, part, chunk, target, rightward)
-        for i in range(group):
-            if i % share == 0:
-                load(step, i // share).wait()
-            which = index_ref[chunk * group + i]
-            real, imag = real_ref[pl.ds(which, 1), :], imag_ref[pl.ds(which, 1), :]
-            band = build_band(real, imag, good_ref[...], block_rows)
-            slab = slab_ref[slot, :, i].reshape(2 * block_rows, channels)
-            both = jnp.dot(band, slab, preferred_element_type=jnp.float32)
-            sum_ref[chunk, i] = both[:total_rows] + both[total_rows:]
+        for piece in range(pieces):
+            load(step, piece).wait()
+            lot = range(piece * share, (piece + 1) * share)
+            for i in lot:
+                which = index_ref[chunk * group + i]
+                real, imag = real_ref[pl.ds(which, 1), :], imag_ref[pl.ds(which, 1), :]
+                band = build_band(real, imag, good_ref[...], block_rows)
+                slab = slab_ref[slot, :, i].reshape(2 * block_rows, channels)
+                both = jnp.dot(band, slab, preferred_element_type=jnp.float32)
+                sum_ref[chunk, i] = both[:total_rows] + both[total_rows:]
+
+            @pl.when(owner != me)
+            def _():
+                start = pl.multiple_of(jnp.where(rightward, far_at, 0), 8)
+                values = [sum_ref[chunk, i, pl.ds(start, 2 * edge), :] for i in lot]
+                encode(values, edge_ref.at[chunk], edge_step_ref.at[chunk, piece], lot[0])
+                edge_copy(chunk, landing, rightward, target, piece).start()
 
         @pl.when(owner != me)
         def _():
-            start = pl.multiple_of(jnp.where(rightward, far_at, 0), 8)
-            values = [sum_ref[chunk, i, pl.ds(start, 2 * edge), :] for i in range(group)]
-            encode(values, edge_ref.at[chunk], edge_step_ref.at[chunk])
-            for copy in edge_copies(chunk, landing, rightward, target):
-                copy.start()
+            edge_step_copy(chunk, landing, target).start()
 
         ends = jnp.logical_and(owner != me, jnp.logical_not(upstream))
 
@@ -366,10 +385,27 @@
         return carry
 
     lax.fori_loop(0, chunks, compute, 0)
+
+    @pl.when(has_left)
+    def _():
+        pl.semaphore_wait(lefts_in, 1)
+
+    @pl.when(has_right)
+    def _():
+        signal(lefts_in, me + 1)
+        pl.semaphore_wait(rights_in, 1)
+
+    @pl.when(has_left)
+    def _():
+        signal(rights_in, me - 1)
+
     forward = chunks - per_owner
 
     def came(slot, start, rows, i):
         return decode(in_ref[slot, pl.ds(start, rows), i])
+
+    def edge_unit(slot, i):
+        return in_edge_step_ref[slot, i // share, :, i % share : i % share + 1]
 
     def pass_mid(step, carry):
         owner, part, chunk = chunk_at(step)
@@ -381,10 +417,9 @@
             for copy in edge_copies(chunk, chunk, rightward, target):
                 copy.wait_recv()
             start = jnp.where(rightward, edge, 0)
-            units = in_edge_step_ref[chunk]
             values = [
                 sum_ref[chunk, i, mid_at : mid_at + 2 * mid, :]
-                + came(chunk, start, mid, i) * units[:, i : i + 1]
+                + came(chunk, start, mid, i) * edge_unit(chunk, i)
                 for i in range(group)
             ]
             encode(values, mid_ref.at[chunk], mid_step_ref.at[chunk])
@@ -411,9 +446,9 @@
             at = lax.broadcasted_iota(jnp.int32, (2 * edge, channels), 0)
             first = jnp.where(rightward, 0, 2 * (edge - mid))
             of_mid = jnp.logical_and(at >= first, at < first + 2 * mid)
-            mids, edges = in_mid_step_ref[chunk], in_edge_step_ref[chunk]
+            mids = in_mid_step_ref[chunk]
             for i in range(group):
-                unit = jnp.where(of_mid, mids[:, i : i + 1], edges[:, i : i + 1])
+                unit = jnp.where(of_mid, mids[:, i : i + 1], edge_unit(chunk, i))
                 value = sum_ref[chunk, i, pl.ds(near, 2 * edge), :]
                 value = value + came(chunk, start, edge, i) * unit
                 done_ref[chunk, :, i] = round_off(value, edge)
@@ -440,15 +475,15 @@
                 copy.wait_recv()
             at = lax.broadcasted_iota(jnp.int32, (2 * edge, channels), 0)
             of_mid = jnp.logical_and(at >= first, at < first + 2 * mid)
-            mids, edges = in_mid_step_ref[slot], in_edge_step_ref[slot]
+            mids = in_mid_step_ref[slot]
             start = edge if rightward else 0
             for i in range(group):
-                unit = jnp.where(of_mid, mids[:, i : i + 1], edges[:, i : i + 1])
+                unit = jnp.where(of_mid, mids[:, i : i + 1], edge_unit(slot, i))
                 sum_ref[chunk, i, near : near + 2 * edge, :] += (
                     came(slot, edge_start, edge, i) * unit
                 )
                 sum_ref[chunk, i, mid_at : mid_at + 2 * mid, :] += (
-                    came(slot, start, mid, i) * edges[:, i : i + 1]
+                    came(slot, start, mid, i) * edge_unit(slot, i)
                 )
 
         @pl.when(has_left)
@@ -544,7 +579,7 @@
     group = GROUP
     while owned % group:
         group //= 2
-    chunks, parts = bases // group, owned // group
+    chunks, parts, pieces = bases // group, owned // group, min(PIECES, group)
     slots = chunks + parts
     small = [
         pltpu.with_memory_space_constraint(operand, pltpu.HBM)
@@ -571,27 +606,29 @@
             pltpu.VMEM((LOADS, block_rows, group, 2, channels), jnp.bfloat16),
             pltpu.VMEM((chunks, group, total_rows, channels), jnp.float32),
             pltpu.VMEM((chunks, edge, group, 2, channels), jnp.int16),
-            pltpu.VMEM((chunks, 1, 128), jnp.float32),
+            pltpu.VMEM((chunks, pieces, 1, 128), jnp.float32),
             pltpu.VMEM((chunks, mid, group, 2, channels), jnp.int16),
             pltpu.VMEM((chunks, 1, 128), jnp.float32),
             pltpu.VMEM((slots, edge + mid, group, 2, channels), jnp.int16),
-            pltpu.VMEM((slots, 1, 128), jnp.float32),
+            pltpu.VMEM((slots, pieces, 1, 128), jnp.float32),
             pltpu.VMEM((slots, 1, 128), jnp.float32),
             pltpu.VMEM((chunks, edge, group, 2, channels), jnp.bfloat16),
             pltpu.VMEM((parts, 2 * edge + mid, group, 2, channels), jnp.bfloat16),
             pltpu.SemaphoreType.DMA((3,)),
-            pltpu.SemaphoreType.DMA((LOADS, 2 if group % 2 == 0 else 1)),
+            pltpu.SemaphoreType.DMA((LOADS, pieces)),
+            pltpu.SemaphoreType.DMA((chunks, pieces)),
             sent,
             sent,
             sent,
-            sent,
-            landed,
+            pltpu.SemaphoreType.DMA((slots, pieces)),
             landed,
             landed,
             landed,
             sent,
             pltpu.SemaphoreType.DMA((count, parts)),
             pltpu.SemaphoreType.DMA((parts,)),
+            pltpu.SemaphoreType.REGULAR,
+            pltpu.SemaphoreType.REGULAR,
         ],
         compiler_params=pltpu.CompilerParams(
             collective_id=0, has_side_effects=True, vmem_limit_bytes=40 * 1024 * 1024

time: 63.8 us -> 63.1 us (0.989)
  Pallas kernels: 62.4 us -> 61.7 us
    pallas_call x1, Pallas kernels: 62.4 us -> 61.7 us  [stream_call(): pl.pallas_call(functools.partial(stream_kernel, count=count), in_specs=[p...]
where the time goes in v5:
time: 63.1 us; the launch traced here: 62.9 us
  Pallas kernels  61.7 us (98%)
  local copies, waits for them, and re-layouts  1.27 us (2%)
    pallas_call x1, Pallas kernels, stream_call(): pl.pallas_call(functools.partial(stream_kernel, count=count), in_specs=[p...  61.7 us
    unnamed x1, local copies, waits for them, and re-layouts  1.27 us

profile of v5, /device:TPU:8, one launch (start us, length us, event | category | flops | bytes accessed | tf_op | source)
XLA Modules:
  0.0 62.9 jit_solution(15043885730308583135)
XLA Ops:
  0.0 61.7 %shard_map.46 = bf16[80,16,2,384]{3,2,1,0:T(2,128)(2,1)S(1)} custom-call(s32[64]{0:T(128)} %index_hbm.1, f32[2,16,257]{2,1,0:T(8,128)} %bank_hbm.1, s32[1,200]{1,0:T(1,128)} %bitcast.1, bf16[200,64,2,384]{3,2,1,0:T(2,128)(2,1)} %vis_ref.1), custom_call_target="tpu_custom_call" | custom-call | tf_op jit(solution)/shard_map/pallas_call | solution.py:589
  61.7 1.3 %copy.6 = bf16[80,16,2,384]{3,2,1,0:T(2,128)(2,1)} copy(bf16[80,16,2,384]{3,2,1,0:T(2,128)(2,1)S(1)} %shard_map.46) | data formatting | bytes 3932160

commit v6 on v5

--- a/solution.py
+++ b/solution.py
@@ -12,7 +12,6 @@
 HALF = TAPS // 2
 SIDE = -(-HALF // AVG)
 GROUP = 8
-PIECES = 2
 LOADS = 3
 LEVELS = 32767.0
 TINY = 1e-33
@@ -80,14 +79,18 @@
     good_ref[...] = spread_flags(flag_ref, flag_matrix)
 
 
-def build_band(real, imag, flags, block_rows):
-    out_count, edge, mid, edge_rows, mid_rows, total_rows, period = row_plan(block_rows)
+def runs_of(block_rows):
+    out_count, edge, mid, edge_rows, mid_rows, _, _ = row_plan(block_rows)
+    return (-SIDE, edge, edge_rows), (out_count - SIDE, mid, mid_rows), (SIDE, edge, edge_rows)
+
+
+def build_band(real, imag, flags, block_rows, runs):
+    period = row_plan(block_rows)[6]
     is_real = lax.broadcasted_iota(jnp.int32, (8, period), 0) % 2 == 0
     tile = jnp.where(
         is_real, jnp.broadcast_to(real, (8, period)), jnp.broadcast_to(imag, (8, period))
     )
     tile = pltpu.roll(tile, 0, 1, stride=AVG, stride_axis=0)
-    runs = ((-SIDE, edge, edge_rows), (out_count - SIDE, mid, mid_rows), (SIDE, edge, edge_rows))
     lanes = round_up(2 * block_rows, 128) + 128
     tiles = []
     for first, count, rows in runs:
@@ -113,6 +116,11 @@
     return jnp.concatenate([high, low], axis=0)
 
 
+def lots_of(group):
+    first = max(3 * group // 8, 1)
+    return [(0, first), (first, group - first)] if group > first else [(0, group)]
+
+
 def encode(values, code_ref, step_ref, first=0):
     lane = lax.broadcasted_iota(jnp.int32, (1, 128), 1)
     steps = jnp.zeros((1, 128), jnp.float32)
@@ -142,6 +150,7 @@
     real_ref,
     imag_ref,
     good_ref,
+    band_ref,
     slab_ref,
     sum_ref,
     edge_ref,
@@ -172,7 +181,7 @@
     count,
 ):
     me = lax.axis_index("tm")
-    _, block_rows, group, _, channels = slab_ref.shape
+    loads, block_rows, group, _, channels = slab_ref.shape
     chunks = done_ref.shape[0]
     per_owner = chunks // count
     out_count, edge, mid, edge_rows, mid_rows, total_rows, _ = row_plan(block_rows)
@@ -191,15 +200,16 @@
         )
         return owner, part, owner * per_owner + part
 
-    pieces = load_sem.shape[1]
-    share = group // pieces
+    lots = lots_of(group)
+    pieces = range(len(lots))
 
     def load(step, piece):
         _, _, chunk = chunk_at(step)
-        slot = step % LOADS
+        slot = step % loads
+        start, size = lots[piece]
         return pltpu.make_async_copy(
-            vis_ref.at[:, pl.ds(chunk * group + piece * share, share)],
-            slab_ref.at[slot, :, pl.ds(piece * share, share)],
+            vis_ref.at[:, pl.ds(chunk * group + start, size)],
+            slab_ref.at[slot, :, pl.ds(start, size)],
             load_sem.at[slot, piece],
         )
 
@@ -219,7 +229,7 @@
 
     def edge_copy(chunk, slot, rightward, device, piece):
         start = jnp.where(rightward, mid, 0)
-        lot = pl.ds(piece * share, share)
+        lot = pl.ds(*lots[piece])
         return remote(
             edge_ref.at[chunk, :, lot],
             in_ref.at[slot, pl.ds(start, edge), lot],
@@ -238,7 +248,7 @@
         )
 
     def edge_copies(chunk, slot, rightward, device):
-        copies = [edge_copy(chunk, slot, rightward, device, piece) for piece in range(pieces)]
+        copies = [edge_copy(chunk, slot, rightward, device, piece) for piece in pieces]
         return copies + [edge_step_copy(chunk, slot, device)]
 
     def mid_copies(chunk, slot, rightward, device):
@@ -299,7 +309,7 @@
     ]
     for copy in smalls:
         copy.start()
-    for piece in range(pieces):
+    for piece in pieces:
         load(0, piece).start()
     def signal(semaphore, device):
         pl.semaphore_signal(
@@ -317,8 +327,8 @@
         signal(barrier, me + 1)
 
     build_rows(bank_ref, flag_ref, real_ref, imag_ref, good_ref, block_rows, smalls)
-    for step in range(1, LOADS - 1):
-        for piece in range(pieces):
+    for step in range(1, loads - 1):
+        for piece in pieces:
             load(step, piece).start()
     pl.semaphore_wait(barrier, has_left.astype(jnp.int32) + has_right.astype(jnp.int32))
 
@@ -327,37 +337,36 @@
         upstream = jnp.where(rightward, has_left, has_right)
         return rightward, upstream, jnp.where(rightward, me + 1, me - 1)
 
-    def compute(step, carry):
-        @pl.when(step + LOADS - 1 < chunks)
-        def _():
-            for piece in range(pieces):
-                load(step + LOADS - 1, piece).start()
-
+    def baseline(chunk, slot, i, band):
+        slab = slab_ref[slot, :, i].reshape(2 * block_rows, channels)
+        both = jnp.dot(band, slab, preferred_element_type=jnp.float32)
+        sum_ref[chunk, i] = both[:total_rows] + both[total_rows:]
+
+    def rows_of(which):
+        return real_ref[pl.ds(which, 1), :], imag_ref[pl.ds(which, 1), :]
+
+    def send_edges(owner, part, chunk, piece):
+        rightward, _, target = flow(owner)
+        landing = slot_of(owner, part, chunk, target, rightward)
+        near = pl.multiple_of(jnp.where(rightward, far_at, 0), 8)
+        start, size = lots[piece]
+        values = [
+            sum_ref[chunk, i, pl.ds(near, 2 * edge), :] for i in range(start, start + size)
+        ]
+        encode(values, edge_ref.at[chunk], edge_step_ref.at[chunk, piece], start)
+        edge_copy(chunk, landing, rightward, target, piece).start()
+        if piece == len(lots) - 1:
+            edge_step_copy(chunk, landing, target).start()
+
+    def prefetch(step):
+        @pl.when(step + loads - 1 < chunks)
+        def _():
+            for piece in pieces:
+                load(step + loads - 1, piece).start()
+
+    def compute_ends(step, carry):
         owner, part, chunk = chunk_at(step)
-        slot = step % LOADS
-        rightward, upstream, target = flow(owner)
-        landing = slot_of(owner, part, chunk, target, rightward)
-        for piece in range(pieces):
-            load(step, piece).wait()
-            lot = range(piece * share, (piece + 1) * share)
-            for i in lot:
-                which = index_ref[chunk * group + i]
-                real, imag = real_ref[pl.ds(which, 1), :], imag_ref[pl.ds(which, 1), :]
-                band = build_band(real, imag, good_ref[...], block_rows)
-                slab = slab_ref[slot, :, i].reshape(2 * block_rows, channels)
-                both = jnp.dot(band, slab, preferred_element_type=jnp.float32)
-                sum_ref[chunk, i] = both[:total_rows] + both[total_rows:]
-
-            @pl.when(owner != me)
-            def _():
-                start = pl.multiple_of(jnp.where(rightward, far_at, 0), 8)
-                values = [sum_ref[chunk, i, pl.ds(start, 2 * edge), :] for i in lot]
-                encode(values, edge_ref.at[chunk], edge_step_ref.at[chunk, piece], lot[0])
-                edge_copy(chunk, landing, rightward, target, piece).start()
-
-        @pl.when(owner != me)
-        def _():
-            edge_step_copy(chunk, landing, target).start()
+        _, upstream, _ = flow(owner)
 
         ends = jnp.logical_and(owner != me, jnp.logical_not(upstream))
 
@@ -384,7 +393,61 @@
 
         return carry
 
-    lax.fori_loop(0, chunks, compute, 0)
+    runs = runs_of(block_rows)
+
+    def first_edges(run, near, rows):
+        def one_chunk(step, carry):
+            owner, part, chunk = chunk_at(step)
+            for piece in pieces:
+                load(step, piece).wait()
+                for i in range(lots[piece][0], sum(lots[piece])):
+                    real, imag = rows_of(index_ref[chunk * group + i])
+                    band = build_band(real, imag, good_ref[...], block_rows, (run,))
+                    slab = slab_ref[step % loads, :, i].reshape(2 * block_rows, channels)
+                    both = jnp.dot(band, slab, preferred_element_type=jnp.float32)
+                    sum_ref[chunk, i, near : near + rows, :] = both[:rows] + both[rows:]
+                send_edges(owner, part, chunk, piece)
+            return carry
+
+        lax.fori_loop(0, per_owner, one_chunk, 0)
+
+    right_first = chunk_at(0)[0] > me
+
+    @pl.when(right_first)
+    def _():
+        first_edges(runs[2], far_at, edge_rows)
+
+    @pl.when(jnp.logical_not(right_first))
+    def _():
+        first_edges(runs[0], 0, edge_rows)
+
+    def one_band(f, carry):
+        band_ref[f] = build_band(*rows_of(f), good_ref[...], block_rows, runs)
+        return carry
+
+    lax.fori_loop(0, real_ref.shape[0], one_band, 0, unroll=2)
+
+    def compute(step, carry):
+        prefetch(step)
+        owner, part, chunk = chunk_at(step)
+        slot = step % loads
+
+        @pl.when(step >= per_owner)
+        def _():
+            for piece in pieces:
+                load(step, piece).wait()
+
+        for i in range(group):
+            baseline(chunk, slot, i, band_ref[index_ref[chunk * group + i]])
+
+        @pl.when(jnp.logical_and(step >= per_owner, owner != me))
+        def _():
+            for piece in pieces:
+                send_edges(owner, part, chunk, piece)
+
+        return carry
+
+    lax.fori_loop(0, chunks, lambda step, carry: compute_ends(step, compute(step, carry)), 0)
 
     @pl.when(has_left)
     def _():
@@ -405,7 +468,9 @@
         return decode(in_ref[slot, pl.ds(start, rows), i])
 
     def edge_unit(slot, i):
-        return in_edge_step_ref[slot, i // share, :, i % share : i % share + 1]
+        piece = [i >= start for start, _ in lots].count(True) - 1
+        lane = i - lots[piece][0]
+        return in_edge_step_ref[slot, piece, :, lane : lane + 1]
 
     def pass_mid(step, carry):
         owner, part, chunk = chunk_at(step)
@@ -579,8 +644,9 @@
     group = GROUP
     while owned % group:
         group //= 2
-    chunks, parts, pieces = bases // group, owned // group, min(PIECES, group)
+    chunks, parts, pieces = bases // group, owned // group, len(lots_of(group))
     slots = chunks + parts
+    loads = max(LOADS, parts + 1)
     small = [
         pltpu.with_memory_space_constraint(operand, pltpu.HBM)
         for operand in (kernel_index, filter_bank, flags)
@@ -603,7 +669,8 @@
             pltpu.VMEM((filters, period), jnp.float32),
             pltpu.VMEM((filters, period), jnp.float32),
             pltpu.VMEM((8, 2 * block_rows), jnp.float32),
-            pltpu.VMEM((LOADS, block_rows, group, 2, channels), jnp.bfloat16),
+            pltpu.VMEM((filters, 2 * total_rows, 2 * block_rows), jnp.bfloat16),
+            pltpu.VMEM((loads, block_rows, group, 2, channels), jnp.bfloat16),
             pltpu.VMEM((chunks, group, total_rows, channels), jnp.float32),
             pltpu.VMEM((chunks, edge, group, 2, channels), jnp.int16),
             pltpu.VMEM((chunks, pieces, 1, 128), jnp.float32),
@@ -615,7 +682,7 @@
             pltpu.VMEM((chunks, edge, group, 2, channels), jnp.bfloat16),
             pltpu.VMEM((parts, 2 * edge + mid, group, 2, channels), jnp.bfloat16),
             pltpu.SemaphoreType.DMA((3,)),
-            pltpu.SemaphoreType.DMA((LOADS, pieces)),
+            pltpu.SemaphoreType.DMA((loads, pieces)),
             pltpu.SemaphoreType.DMA((chunks, pieces)),
             sent,
             sent,

time: 63.1 us -> 62.7 us (level)
  no operation moved by 1% of the time
where the time goes in v6:
time: 62.7 us; the launch traced here: 62.6 us
  Pallas kernels  61.3 us (98%)
  local copies, waits for them, and re-layouts  1.27 us (2%)
    pallas_call x1, Pallas kernels, stream_call(): pl.pallas_call(functools.partial(stream_kernel, count=count), in_specs=[p...  61.3 us
    unnamed x1, local copies, waits for them, and re-layouts  1.27 us

profile of v6, /device:TPU:8, one launch (start us, length us, event | category | flops | bytes accessed | tf_op | source)
XLA Modules:
  0.0 62.6 jit_solution(8811938212384271554)
XLA Ops:
  0.0 61.3 %shard_map.46 = bf16[80,16,2,384]{3,2,1,0:T(2,128)(2,1)S(1)} custom-call(s32[64]{0:T(128)} %index_hbm.1, f32[2,16,257]{2,1,0:T(8,128)} %bank_hbm.1, s32[1,200]{1,0:T(1,128)} %bitcast.1, bf16[200,64,2,384]{3,2,1,0:T(2,128)(2,1)} %vis_ref.1), custom_call_target="tpu_custom_call" | custom-call | tf_op jit(solution)/shard_map/pallas_call | solution.py:655
  61.3 1.3 %copy.6 = bf16[80,16,2,384]{3,2,1,0:T(2,128)(2,1)} copy(bf16[80,16,2,384]{3,2,1,0:T(2,128)(2,1)S(1)} %shard_map.46) | data formatting | bytes 3932160

commit v7 on v6

--- a/solution.py
+++ b/solution.py
@@ -330,7 +330,6 @@
     for step in range(1, loads - 1):
         for piece in pieces:
             load(step, piece).start()
-    pl.semaphore_wait(barrier, has_left.astype(jnp.int32) + has_right.astype(jnp.int32))
 
     def flow(owner):
         rightward = owner > me
@@ -406,6 +405,13 @@
                     slab = slab_ref[step % loads, :, i].reshape(2 * block_rows, channels)
                     both = jnp.dot(band, slab, preferred_element_type=jnp.float32)
                     sum_ref[chunk, i, near : near + rows, :] = both[:rows] + both[rows:]
+                if piece == 0:
+
+                    @pl.when(step == 0)
+                    def _():
+                        greeted = has_left.astype(jnp.int32) + has_right.astype(jnp.int32)
+                        pl.semaphore_wait(barrier, greeted)
+
                 send_edges(owner, part, chunk, piece)
             return carry
 

time: 62.7 us -> 62.6 us (level)
  no operation moved by 1% of the time
where the time goes in v7:
time: 62.6 us; the launch traced here: 62.5 us
  Pallas kernels  61.2 us (98%)
  local copies, waits for them, and re-layouts  1.27 us (2%)
    pallas_call x1, Pallas kernels, stream_call(): pl.pallas_call(functools.partial(stream_kernel, count=count), in_specs=[p...  61.2 us
    unnamed x1, local copies, waits for them, and re-layouts  1.27 us

profile of v7, /device:TPU:8, one launch (start us, length us, event | category | flops | bytes accessed | tf_op | source)
XLA Modules:
  0.0 62.5 jit_solution(2426049927413538447)
XLA Ops:
  0.0 61.2 %shard_map.46 = bf16[80,16,2,384]{3,2,1,0:T(2,128)(2,1)S(1)} custom-call(s32[64]{0:T(128)} %index_hbm.1, f32[2,16,257]{2,1,0:T(8,128)} %bank_hbm.1, s32[1,200]{1,0:T(1,128)} %bitcast.1, bf16[200,64,2,384]{3,2,1,0:T(2,128)(2,1)} %vis_ref.1), custom_call_target="tpu_custom_call" | custom-call | tf_op jit(solution)/shard_map/pallas_call | solution.py:661
  61.2 1.3 %copy.6 = bf16[80,16,2,384]{3,2,1,0:T(2,128)(2,1)} copy(bf16[80,16,2,384]{3,2,1,0:T(2,128)(2,1)S(1)} %shard_map.46) | data formatting | bytes 3932160
